TPU v7x, 32 devices: a whole 2x2x4 slice. The times are simulated.
32 devices in a mesh: expert: 16 (over z, y, x), dp: 2 (over core).
Axes of the slice: x: 2, y: 2, z: 4, core: 2. Of those that a mesh axis runs over, the one named last changes fastest.
Arguments:
- tokens: bfloat16 [8192, 4096], P('expert', 'dp'), may hold values from -6 to 6
- cotangent: bfloat16 [8192, 4096], P('expert', 'dp'), may hold values from -6 to 6
- routes: int32 [8192, 8], P('expert'), may hold values from 0 to 15, all different within a row; in each aligned block of 512 rows (0 to 511, 512 to 1023, ...) at most 512 rows name the same one
- probs: bfloat16 [8192, 8], P('expert'), may hold values from 0.099609375 to 1
- expert_slot: int32 [16], replicated, may hold values from 0 to 15, each once
- pull_flags: int32 [16], replicated, may hold values 0 or 1
- w_gate: bfloat16 [16, 768, 4096], P('expert', None, 'dp'), may hold values from -0.09375 to 0.09375
- w_up: bfloat16 [16, 768, 4096], P('expert', None, 'dp'), may hold values from -0.09375 to 0.09375
- w_down: bfloat16 [16, 768, 4096], P('expert', None, 'dp'), may hold values from -0.21875 to 0.21875
Outputs:
- expert_out: bfloat16 [8192, 4096], P('expert', 'dp')
- token_grad: bfloat16 [8192, 4096], P('expert', 'dp')
- gate_grad: bfloat16 [16, 768, 4096], P('expert', None, 'dp')
- up_grad: bfloat16 [16, 768, 4096], P('expert', None, 'dp')
- down_grad: bfloat16 [16, 768, 4096], P('expert', None, 'dp')
Inputs may be any that keep to these rules, and one draw needn't show every extreme that they name: `routes`: each row names 8 different experts. Within the 512 rows of one token batch no expert is named by more than 512 rows, and in some batch some expert is named by exactly 512 rows. `expert_slot`: A permutation of the experts.
All inputs are finite; a program needn't handle non-finite values.
Results may differ from a plain program's by a relative error of at most 0.006.
Values may be sent and summed in bfloat16 or wider, within the bound.
No kernel may reach another device: no remote copies, remote signals or barrier semaphores. Data moves between devices by JAX's collectives and lax.ppermute only.
A program may use at most 128 MiB of HBM per device.

v0:
```python
import jax
import jax.numpy as jnp
from jax import lax
from jax.sharding import PartitionSpec as P


def passed_along(value, axis, steps):
    count = lax.axis_size(axis)
    pairs = [(source, (source + steps) % count) for source in range(count)]
    return lax.ppermute(value, axis, pairs)


def silu_parts(gate_val):
    sigmoid_val = jax.nn.sigmoid(gate_val)
    return (gate_val * sigmoid_val, sigmoid_val * (1.0 + gate_val * (1.0 - sigmoid_val)))


def slot_rows(route_ids, weights_in, expert, scale, capacity):
    count = route_ids.shape[0]
    hit = route_ids == expert
    member = jnp.any(hit, axis=1)
    weight = jnp.sum(jnp.where(hit, weights_in.astype(jnp.float32), 0.0), axis=1) * scale
    rank = jnp.cumsum(member.astype(jnp.int32), dtype=jnp.int32) - 1
    entries = jnp.arange(capacity, dtype=jnp.int32)
    chosen = member[None, :] & (rank[None, :] == entries[:, None])
    positions = jnp.arange(count, dtype=jnp.int32)
    index = jnp.sum(jnp.where(chosen, positions[None, :], 0), axis=1, dtype=jnp.int32)
    index = jnp.where(jnp.any(chosen, axis=1), index, count)
    return (index, jnp.take(weight, index, mode="fill", fill_value=0.0))


def hidden_values(gate_val, up_val, back_val, rows_w):
    activated, slope_val = silu_parts(gate_val)
    weight_col = rows_w[..., None]
    scaled = (weight_col * activated * up_val).astype(jnp.bfloat16)
    grad_gate = (back_val * weight_col * up_val * slope_val).astype(jnp.bfloat16)
    grad_up = (back_val * weight_col * activated).astype(jnp.bfloat16)
    return (scaled, grad_gate, grad_up)


def take_rows(array, index):
    return jnp.take(array, index, axis=0, mode="fill", fill_value=0)


def finish_set(scaled, grad_gate, grad_up, rows_x, rows_dy, wg, wu, wd):
    out_rows = jnp.dot(scaled, wd, preferred_element_type=jnp.float32)
    in_rows = jnp.dot(grad_gate, wg, preferred_element_type=jnp.float32)
    in_rows = in_rows + jnp.dot(grad_up, wu, preferred_element_type=jnp.float32)
    over_rows = (((0,), (0,)), ((), ()))
    grad_terms = (
        lax.dot_general(grad_gate, rows_x, over_rows, preferred_element_type=jnp.float32),
        lax.dot_general(grad_up, rows_x, over_rows, preferred_element_type=jnp.float32),
        lax.dot_general(scaled, rows_dy, over_rows, preferred_element_type=jnp.float32),
    )
    return (out_rows, in_rows, tuple((term.astype(jnp.bfloat16) for term in grad_terms)))


def per_device(tokens, cotangent, routes, probs, expert_slot, pull_flags, w_gate, w_up, w_down):
    columns = lax.axis_size("expert")
    column = lax.axis_index("expert")
    count = tokens.shape[0]
    capacity = min(count, count * routes.shape[1] * 2 // columns)
    labels = jnp.arange(columns, dtype=jnp.int32)
    following = (column + 1) % columns

    def owner_expert(slot):
        return jnp.sum(jnp.where(expert_slot == slot, labels, 0), dtype=jnp.int32)

    flag = pull_flags[column].astype(jnp.float32)
    own_index, own_weight = slot_rows(routes, probs, owner_expert(column), 1.0, capacity)
    next_index, next_weight = slot_rows(routes, probs, owner_expert(following), flag, capacity)
    own_x = take_rows(tokens, own_index)
    own_dy = take_rows(cotangent, own_index)
    next_x = take_rows(tokens, next_index)
    next_dy = take_rows(cotangent, next_index)
    own_set = (own_x, own_dy, own_weight, w_gate[0], w_up[0], w_down[0])
    arrived = passed_along((next_x, next_dy, next_weight.astype(jnp.bfloat16)), "expert", 1)
    far_set = (
        arrived[0],
        arrived[1],
        arrived[2].astype(jnp.float32),
        w_gate[0],
        w_up[0],
        w_down[0],
    )
    both_sets = (own_set, far_set)
    contract = (((1,), (1,)), ((), ()))
    partial_gate = jnp.stack(
        [
            lax.dot_general(one[0], one[3], contract, preferred_element_type=jnp.float32)
            for one in both_sets
        ]
    )
    partial_up = jnp.stack(
        [
            lax.dot_general(one[0], one[4], contract, preferred_element_type=jnp.float32)
            for one in both_sets
        ]
    )
    partial_back = jnp.stack(
        [
            lax.dot_general(one[1], one[5], contract, preferred_element_type=jnp.float32)
            for one in both_sets
        ]
    )
    gate_val, up_val, back_val = (
        lax.psum_scatter(partial_gate, "dp", scatter_dimension=2, tiled=True),
        lax.psum_scatter(partial_up, "dp", scatter_dimension=2, tiled=True),
        lax.psum_scatter(partial_back, "dp", scatter_dimension=2, tiled=True),
    )
    rows_w = jnp.stack([own_set[2], far_set[2]])
    scaled, grad_gate, grad_up = hidden_values(gate_val, up_val, back_val, rows_w)
    scaled, grad_gate, grad_up = (
        lax.all_gather(scaled, "dp", axis=2, tiled=True),
        lax.all_gather(grad_gate, "dp", axis=2, tiled=True),
        lax.all_gather(grad_up, "dp", axis=2, tiled=True),
    )
    own_out, own_in, own_grads = finish_set(
        scaled[0],
        grad_gate[0],
        grad_up[0],
        own_set[0],
        own_set[1],
        own_set[3],
        own_set[4],
        own_set[5],
    )
    far_out, far_in, far_grads = finish_set(
        scaled[1],
        grad_gate[1],
        grad_up[1],
        far_set[0],
        far_set[1],
        far_set[3],
        far_set[4],
        far_set[5],
    )
    next_out, next_in = (
        passed_along(far_out.astype(jnp.bfloat16), "expert", -1).astype(far_out.dtype),
        passed_along(far_in.astype(jnp.bfloat16), "expert", -1).astype(far_in.dtype),
    )
    grad_sums = tuple(
        (
            (
                lax.optimization_barrier(mine).astype(jnp.float32)
                + lax.optimization_barrier(theirs).astype(jnp.float32)
            ).astype(jnp.bfloat16)
            for mine, theirs in zip(own_grads, far_grads)
        )
    )
    empty = jnp.zeros(tokens.shape, jnp.float32)
    out_part = (
        empty.at[own_index].add(own_out, mode="drop").at[next_index].add(next_out, mode="drop")
    )
    in_part = empty.at[own_index].add(own_in, mode="drop").at[next_index].add(next_in, mode="drop")
    return (
        out_part.astype(jnp.bfloat16),
        in_part.astype(jnp.bfloat16),
        grad_sums[0][None],
        grad_sums[1][None],
        grad_sums[2][None],
    )


def solution(mesh):
    return jax.shard_map(
        per_device,
        mesh=mesh,
        in_specs=(
            P("expert", "dp"),
            P("expert", "dp"),
            P("expert", None),
            P("expert", None),
            P(),
            P(),
            P("expert", None, "dp"),
            P("expert", None, "dp"),
            P("expert", None, "dp"),
        ),
        out_specs=(
            P("expert", "dp"),
            P("expert", "dp"),
            P("expert", None, "dp"),
            P("expert", None, "dp"),
            P("expert", None, "dp"),
        ),
        check_vma=False,
    )
```

profile of v0, /device:TPU:0, one launch (start us, length us, event | category | flops | bytes accessed | tf_op | source)
XLA Modules:
  0.0 333.3 jit_solution(14110842430651859816)
XLA Ops:
  7.2 1.4 fusion.67
  8.7 2.0 fusion.64
  11.9 7.1 %gather_fusion.5 = bf16[512,2048]{1,0:T(8,128)(2,1)} fusion(bf16[512,2048]{1,0:T(8,128)(2,1)} %param.14, s32[1024]{0:T(1024)S(1)} %pad_clamp_fusion), kind=kCustom, calls=%fused_computation.5.clone | custom fusion | bytes 4196352 | tf_op jit(solution)/shard_map/jit(_take)/gather | solution.py:42
  19.0 7.1 %gather_fusion.3 = bf16[512,2048]{1,0:T(8,128)(2,1)} fusion(bf16[512,2048]{1,0:T(8,128)(2,1)} %param.13, s32[1024]{0:T(1024)S(1)} %pad_clamp_fusion), kind=kCustom, calls=%fused_computation.3.clone | custom fusion | bytes 4196352 | tf_op jit(solution)/shard_map/jit(_take)/gather | solution.py:42
  27.4 3.5 %gather_fusion.1 = bf16[512]{0:T(512)(128)(2,1)S(1)} fusion(bf16[512]{0:T(512)(128)(2,1)S(1)} %broadcast_multiply_fusion, s32[1024]{0:T(1024)S(1)} %pad_clamp_fusion), kind=kCustom, calls=%fused_computation.2.clone | custom fusion | bytes 4096 | tf_op jit(solution)/shard_map/jit(_take)/gather | solution.py:29
  30.9 4.6 %broadcast_select_fusion = (bf16[512,2048]{1,0:T(8,128)(2,1)}, bf16[512,2048]{1,0:T(8,128)(2,1)}) fusion(bf16[512,2048]{1,0:T(8,128)(2,1)} %gather_fusion.5, pred[512]{0:T(512)(128)(4,1)S(1)} %get-tuple-element.14, bf16[512,2048]{1,0:T(8,128)(2,1)} %gather_fusion.3), kind=kLoop, calls=%fused_computation.60 | loop fusion | flops 2097152 | bytes 8389120 | tf_op jit(solution)/shard_map/jit(_take)/select_n | solution.py:42
  35.5 3.1 collective-permute-start.1
  39.8 7.1 %gather_fusion.2 = bf16[512,2048]{1,0:T(8,128)(2,1)} fusion(bf16[512,2048]{1,0:T(8,128)(2,1)} %param.13, s32[1024]{0:T(1024)S(1)} %pad_clamp_fusion.1), kind=kCustom, calls=%fused_computation.1.clone | custom fusion | bytes 4196352 | tf_op jit(solution)/shard_map/jit(_take)/gather | solution.py:42
  46.9 3.5 %gather_fusion = f32[512]{0:T(512)S(1)} fusion(f32[512]{0:T(512)S(1)} %get-tuple-element.7, s32[1024]{0:T(1024)S(1)} %pad_clamp_fusion.1), kind=kCustom, calls=%fused_computation.clone | custom fusion | bytes 6144 | tf_op jit(solution)/shard_map/jit(_take)/gather | solution.py:29
  50.4 4.5 %fusion.42 = f32[1,512,768]{2,1,0:T(8,128)S(1)} fusion(bf16[1,768,2048]{2,1,0:T(8,128)(2,1)} %param.19, bf16[512,2048]{1,0:T(8,128)(2,1)} %gather_fusion.2, pred[512]{0:T(512)(128)(4,1)S(1)} %get-tuple-element.12), kind=kOutput, calls=%fused_computation.69 | convolution fusion | flops 1611661312 | bytes 6816256 | tf_op jit(solution)/shard_map/dot_general | solution.py:90
  54.9 33.6 %collective-permute-done.1 = bf16[512,2048]{1,0:T(8,128)(2,1)} collective-permute-done((bf16[512,2048]{1,0:T(8,128)(2,1)}, bf16[512,2048]{1,0:T(8,128)(2,1)}, u32[]{:S(2)}, u32[]{:S(2)}) %collective-permute-start.1) | collective-permute-done | bytes 2097184 | tf_op jit(solution)/shard_map/ppermute | solution.py:10
  88.5 3.4 %fusion.45 = f32[1,512,768]{2,1,0:T(8,128)S(1)} fusion(bf16[512,2048]{1,0:T(8,128)(2,1)} %collective-permute-done.1, bf16[1,768,2048]{2,1,0:T(8,128)(2,1)S(1)} %copy-done.7), kind=kOutput, calls=%fused_computation.70 | convolution fusion | flops 1610612736 | bytes 6815744 | tf_op jit(solution)/shard_map/dot_general | solution.py:90
  92.0 1.9 pad_maximum_fusion
  93.9 3.4 %fusion.48 = f32[1,512,768]{2,1,0:T(8,128)S(1)} fusion(bf16[1,768,2048]{2,1,0:T(8,128)(2,1)S(1)} %copy-done, bf16[512,2048]{1,0:T(8,128)(2,1)} %gather_fusion.2, pred[512]{0:T(512)(128)(4,1)S(1)} %get-tuple-element.12), kind=kOutput, calls=%fused_computation.71 | convolution fusion | flops 1611661312 | bytes 6816256 | tf_op jit(solution)/shard_map/dot_general | solution.py:96
  97.4 3.6 %fusion.51 = f32[1,512,768]{2,1,0:T(8,128)S(1)} fusion(bf16[512,2048]{1,0:T(8,128)(2,1)} %collective-permute-done.1, bf16[1,768,2048]{2,1,0:T(8,128)(2,1)S(1)} %copy-done), kind=kOutput, calls=%fused_computation.72 | convolution fusion | flops 1610612736 | bytes 6815744 | tf_op jit(solution)/shard_map/dot_general | solution.py:96
  100.9 1.9 pad_maximum_fusion.1
  103.2 7.1 %gather_fusion.4 = bf16[512,2048]{1,0:T(8,128)(2,1)} fusion(bf16[512,2048]{1,0:T(8,128)(2,1)} %param.14, s32[1024]{0:T(1024)S(1)} %pad_clamp_fusion.1), kind=kCustom, calls=%fused_computation.4.clone | custom fusion | bytes 4196352 | tf_op jit(solution)/shard_map/jit(_take)/gather | solution.py:42
  110.3 4.9 %fusion.54 = f32[1,512,768]{2,1,0:T(8,128)S(1)} fusion(bf16[1,768,2048]{2,1,0:T(8,128)(2,1)} %param.21, bf16[512,2048]{1,0:T(8,128)(2,1)} %gather_fusion.4, pred[512]{0:T(512)(128)(4,1)S(1)} %get-tuple-element.12), kind=kOutput, calls=%fused_computation.73 | convolution fusion | flops 1611661312 | bytes 6816256 | tf_op jit(solution)/shard_map/dot_general | solution.py:102
  115.2 38.9 %collective-permute-done.3 = bf16[512,2048]{1,0:T(8,128)(2,1)} collective-permute-done((bf16[512,2048]{1,0:T(8,128)(2,1)}, bf16[512,2048]{1,0:T(8,128)(2,1)}, u32[]{:S(2)}, u32[]{:S(2)}) %collective-permute-start.3) | collective-permute-done | bytes 2097184 | tf_op jit(solution)/shard_map/ppermute | solution.py:10
  154.2 3.4 %fusion.57 = f32[1,512,768]{2,1,0:T(8,128)S(1)} fusion(bf16[512,2048]{1,0:T(8,128)(2,1)} %collective-permute-done.3, bf16[1,768,2048]{2,1,0:T(8,128)(2,1)S(1)} %copy-done.9), kind=kOutput, calls=%fused_computation.74 | convolution fusion | flops 1610612736 | bytes 6815744 | tf_op jit(solution)/shard_map/dot_general | solution.py:102
  157.6 1.9 pad_maximum_fusion.2
  159.6 7.2 %collective-permute-done = bf16[512]{0:T(512)(128)(2,1)S(1)} collective-permute-done((bf16[512]{0:T(512)(128)(2,1)S(1)}, bf16[512]{0:T(512)(128)(2,1)S(1)}, u32[]{:S(2)}, u32[]{:S(2)}) %collective-permute-start) | collective-permute-done | bytes 1056 | tf_op jit(solution)/shard_map/ppermute | solution.py:10
  166.9 4.7 %multiply_convert_fusion = (bf16[2,512,384]{2,1,0:T(8,128)(2,1)}, bf16[2,512,384]{2,1,0:T(8,128)(2,1)}, bf16[2,512,384]{2,1,0:T(8,128)(2,1)}) fusion(f32[2,512,384]{2,1,0:T(8,128)} %reduce-scatter.8.cloned.1.call-done, f32[2,512]{1,0:T(2,128)S(1)} %pad_maximum_fusion.3, f32[2,512,384]{2,1,0:T(8,128)} %reduce-scatter.4.cloned.1.call-done, ...), kind=kLoop, calls=%fused_computation.64 | loop fusion | flops 6684672 | bytes 7081984 | tf_op jit(solution)/shard_map/convert_element_type | solution.py:37
  172.7 9.6 %all-gather.8.cloned.1.call-done = bf16[2,512,768]{2,1,0:T(8,128)(2,1)} async-done(((bf16[2,512,384]{2,1,0:T(8,128)(2,1)}), bf16[2,512,768]{2,1,0:T(8,128)(2,1)}) %all-gather.8.cloned.1.call-update) | async-done | bytes 1572880 | tf_op jit(solution)/shard_map/all_gather | solution.py:116
  182.4 4.9 %fusion.17 = f32[512,2048]{1,0:T(8,128)} fusion(bf16[1,768,2048]{2,1,0:T(8,128)(2,1)S(1)} %copy-done, bf16[2,512,768]{2,1,0:T(8,128)(2,1)} %all-gather.8.cloned.1.call-done), kind=kOutput, calls=%fused_computation.40 | convolution fusion | flops 1610612736 | bytes 8126464 | tf_op jit(solution)/shard_map/dot_general | solution.py:48
  187.2 8.1 %all-gather.6.cloned.1.call-done = bf16[2,512,768]{2,1,0:T(8,128)(2,1)} async-done(((bf16[2,512,384]{2,1,0:T(8,128)(2,1)}), bf16[2,512,768]{2,1,0:T(8,128)(2,1)}) %all-gather.6.cloned.1.call-update) | async-done | bytes 1572880 | tf_op jit(solution)/shard_map/all_gather | solution.py:115
  195.3 6.5 %add_convert_fusion.3 = bf16[512,2048]{1,0:T(8,128)(2,1)} fusion(f32[512,2048]{1,0:T(8,128)} %fusion.17, bf16[1,768,2048]{2,1,0:T(8,128)(2,1)} %param.19, bf16[2,512,768]{2,1,0:T(8,128)(2,1)} %all-gather.6.cloned.1.call-done), kind=kOutput, calls=%fused_computation.15 | convolution fusion | flops 1612709888 | bytes 10223616 | tf_op jit(solution)/shard_map/dot_general | solution.py:47
  201.8 5.4 %collective-permute-start.4 = (bf16[512,2048]{1,0:T(8,128)(2,1)}, bf16[512,2048]{1,0:T(8,128)(2,1)}, u32[]{:S(2)}, u32[]{:S(2)}) collective-permute-start(bf16[512,2048]{1,0:T(8,128)(2,1)} %add_convert_fusion.3), channel_id=1, source_target_pairs={{0,30},{2,0},{4,2},{6,4},{8,6},{10,8},{12,10},{14,12},{16,14},{18,... | collective-permute-start | bytes 6291464 | tf_op jit(solution)/shard_map/ppermute | solution.py:10
  208.2 5.3 %fusion.33 = bf16[512,2048]{1,0:T(8,128)(2,1)} fusion(bf16[1,768,2048]{2,1,0:T(8,128)(2,1)} %param.21, bf16[2,512,768]{2,1,0:T(8,128)(2,1)} %all-gather.4.cloned.1.call-done), kind=kOutput, calls=%fused_computation.56 | convolution fusion | flops 1611661312 | bytes 6029312 | tf_op jit(solution)/shard_map/dot_general | solution.py:46
  213.6 5.8 %collective-permute-start.2 = (bf16[512,2048]{1,0:T(8,128)(2,1)}, bf16[512,2048]{1,0:T(8,128)(2,1)}, u32[]{:S(2)}, u32[]{:S(2)}) collective-permute-start(bf16[512,2048]{1,0:T(8,128)(2,1)} %fusion.33), channel_id=1, source_target_pairs={{0,30},{2,0},{4,2},{6,4},{8,6},{10,8},{12,10},{14,12},{16,14},{18,... | collective-permute-start | bytes 6291464 | tf_op jit(solution)/shard_map/ppermute | solution.py:10
  219.4 5.1 %convolution_convert_fusion.2 = bf16[768,2048]{1,0:T(8,128)(2,1)} fusion(bf16[512,2048]{1,0:T(8,128)(2,1)} %collective-permute-done.1, bf16[2,512,768]{2,1,0:T(8,128)(2,1)S(1)} %copy-done.11), kind=kOutput, calls=%fused_computation.22 | convolution fusion | flops 1612185600 | bytes 6029312 | tf_op jit(solution)/shard_map/dot_general | solution.py:52
  224.5 3.6 %convolution_convert_fusion.3 = bf16[768,2048]{1,0:T(8,128)(2,1)} fusion(bf16[2,512,768]{2,1,0:T(8,128)(2,1)S(1)} %copy-done.11, bf16[512,2048]{1,0:T(8,128)(2,1)S(1)} %copy-done.5, pred[512]{0:T(512)(128)(4,1)S(1)} %get-tuple-element.12), kind=kOutput, calls=%fused_computation.23 | convolution fusion | flops 1613234176 | bytes 6029824 | tf_op jit(solution)/shard_map/dot_general | solution.py:52
  228.0 5.2 %convolution_convert_fusion = bf16[768,2048]{1,0:T(8,128)(2,1)} fusion(bf16[512,2048]{1,0:T(8,128)(2,1)} %collective-permute-done.3, bf16[2,512,768]{2,1,0:T(8,128)(2,1)S(1)} %copy-done.13), kind=kOutput, calls=%fused_computation.20 | convolution fusion | flops 1612185600 | bytes 6029312 | tf_op jit(solution)/shard_map/dot_general | solution.py:53
  233.3 3.6 %convolution_convert_fusion.1 = bf16[768,2048]{1,0:T(8,128)(2,1)} fusion(bf16[512,2048]{1,0:T(8,128)(2,1)S(1)} %copy-done.6, pred[512]{0:T(512)(128)(4,1)S(1)} %get-tuple-element.12, bf16[2,512,768]{2,1,0:T(8,128)(2,1)S(1)} %copy-done.13), kind=kOutput, calls=%fused_computation.21 | convolution fusion | flops 1613234176 | bytes 6029824 | tf_op jit(solution)/shard_map/dot_general | solution.py:53
  236.9 3.6 %convolution_convert_fusion.5 = bf16[768,2048]{1,0:T(8,128)(2,1)} fusion(bf16[2,512,768]{2,1,0:T(8,128)(2,1)S(1)} %copy-done.12, bf16[512,2048]{1,0:T(8,128)(2,1)S(1)} %copy-done.5, pred[512]{0:T(512)(128)(4,1)S(1)} %get-tuple-element.12), kind=kOutput, calls=%fused_computation.25 | convolution fusion | flops 1613234176 | bytes 6029824 | tf_op jit(solution)/shard_map/dot_general | solution.py:51
  240.5 3.8 %fusion.19 = f32[512,2048]{1,0:T(8,128)} fusion(bf16[1,768,2048]{2,1,0:T(8,128)(2,1)S(1)} %copy-done, bf16[2,512,768]{2,1,0:T(8,128)(2,1)S(1)} %copy-done.11), kind=kOutput, calls=%fused_computation.42 | convolution fusion | flops 1610612736 | bytes 8126464 | tf_op jit(solution)/shard_map/dot_general | solution.py:48
  244.2 3.8 %fusion.27 = f32[512,2048]{1,0:T(8,128)} fusion(bf16[1,768,2048]{2,1,0:T(8,128)(2,1)S(1)} %copy-done.8, bf16[2,512,768]{2,1,0:T(8,128)(2,1)S(1)} %copy-done.12), kind=kOutput, calls=%fused_computation.50 | convolution fusion | flops 1610612736 | bytes 8126464 | tf_op jit(solution)/shard_map/dot_general | solution.py:47
  248.0 3.8 %fusion.15 = f32[512,2048]{1,0:T(8,128)} fusion(bf16[1,768,2048]{2,1,0:T(8,128)(2,1)S(1)} %copy-done.10, bf16[2,512,768]{2,1,0:T(8,128)(2,1)S(1)} %copy-done.13), kind=kOutput, calls=%fused_computation.38 | convolution fusion | flops 1610612736 | bytes 8126464 | tf_op jit(solution)/shard_map/dot_general | solution.py:46
  251.8 5.3 %convolution_convert_fusion.4 = bf16[768,2048]{1,0:T(8,128)(2,1)} fusion(bf16[512,2048]{1,0:T(8,128)(2,1)} %collective-permute-done.1, bf16[2,512,768]{2,1,0:T(8,128)(2,1)S(1)} %copy-done.12), kind=kOutput, calls=%fused_computation.24 | convolution fusion | flops 1612185600 | bytes 6029312 | tf_op jit(solution)/shard_map/dot_general | solution.py:51
  257.1 10.8 %scatter_custom_fusion = f32[512,2048]{1,0:T(8,128)} fusion(s32[512]{0:T(512)S(1)} %bitcast.112, f32[512,2048]{1,0:T(8,128)} %fusion.15, f32[]{:T(128)} %constant.31.clone.1), kind=kCustom, calls=%fused_computation.58 | custom fusion | flops 1048576 | bytes 4194816 | tf_op jit(solution)/shard_map/scatter-add | solution.py:153
  267.9 12.6 %scatter_custom_fusion.2 = f32[512,2048]{1,0:T(8,128)} fusion(s32[512]{0:T(512)S(1)} %bitcast.113, f32[512,2048]{1,0:T(8,128)} %fusion.27, f32[512,2048]{1,0:T(8,128)} %fusion.19, f32[]{:T(128)} %constant.31.clone.1), kind=kCustom, calls=%fused_computation.16 | custom fusion | flops 2097152 | bytes 12582916 | tf_op jit(solution)/shard_map/scatter-add | solution.py:155
  280.5 6.2 %fusion.7 = bf16[1,768,2048]{2,1,0:T(8,128)(2,1)} fusion(bf16[768,2048]{1,0:T(8,128)(2,1)} %convolution_convert_fusion.2, bf16[768,2048]{1,0:T(8,128)(2,1)} %convolution_convert_fusion.3), kind=kLoop, calls=%fused_computation.27 | loop fusion | flops 6291456 | bytes 9437184 | tf_op jit(solution)/shard_map/broadcast_in_dim | solution.py:160
  286.7 3.1 fusion.8
  290.5 3.1 fusion.6
  293.6 12.5 %scatter_custom_fusion.3 = f32[512,2048]{1,0:T(8,128)} fusion(f32[512,2048]{1,0:T(8,128)} %scatter_custom_fusion.2, s32[512]{0:T(512)S(1)} %bitcast.110, bf16[512,2048]{1,0:T(8,128)(2,1)} %collective-permute-done.4), kind=kCustom, calls=%fused_computation.13 | custom fusion | flops 2097152 | bytes 6291456 | tf_op jit(solution)/shard_map/scatter-add | solution.py:155
  306.1 3.8 %convert_element_type.116 = bf16[512,2048]{1,0:T(8,128)(2,1)} convert(f32[512,2048]{1,0:T(8,128)} %scatter_custom_fusion.3) | non-fusion elementwise | flops 1048576 | bytes 6291456 | tf_op jit(solution)/shard_map/convert_element_type | solution.py:158
  310.0 12.2 %scatter_custom_fusion.1 = f32[512,2048]{1,0:T(8,128)} fusion(f32[512,2048]{1,0:T(8,128)} %scatter_custom_fusion, s32[512]{0:T(512)S(1)} %bitcast.111, bf16[512,2048]{1,0:T(8,128)(2,1)} %collective-permute-done.2), kind=kCustom, calls=%fused_computation.18 | custom fusion | flops 2097152 | bytes 6291456 | tf_op jit(solution)/shard_map/scatter-add | solution.py:153
  322.1 3.8 %convert_element_type.111 = bf16[512,2048]{1,0:T(8,128)(2,1)} convert(f32[512,2048]{1,0:T(8,128)} %scatter_custom_fusion.1) | non-fusion elementwise | flops 1048576 | bytes 6291456 | tf_op jit(solution)/shard_map/convert_element_type | solution.py:157
  (80 shorter events, 6.5 us)
Async XLA Ops:
  7.2 86.8 %copy-start = (bf16[1,768,2048]{2,1,0:T(8,128)(2,1)S(1)}, bf16[1,768,2048]{2,1,0:T(8,128)(2,1)}, u32[]{:S(2)}) copy-start(bf16[1,768,2048]{2,1,0:T(8,128)(2,1)} %param.20) | copy-start | bytes 9437188
  7.2 159.6 %reduce-scatter.4.cloned.1.call-start = ((), (), s32[]{:S(2)}) async-start(), calls=%async_computation.3 | async-start | bytes 4718592 | tf_op jit(solution)/shard_map/reduce_scatter | solution.py:107
  19.0 7.1 %copy-start.14 = (s32[16]{0:T(128)S(1)}, s32[16]{0:T(128)}, u32[]{:S(2)}) copy-start(s32[16]{0:T(128)} %param.18) | copy-start | bytes 196
  35.5 53.1 %collective-permute-start.1 = (bf16[512,2048]{1,0:T(8,128)(2,1)}, bf16[512,2048]{1,0:T(8,128)(2,1)}, u32[]{:S(2)}, u32[]{:S(2)}) collective-permute-start(bf16[512,2048]{1,0:T(8,128)(2,1)} %get-tuple-element.25), channel_id=1, source_target_pairs={{0,2},{2,4},{4,6},{6,8},{8,10},{10,12},{12,14},{14,16},{16,18},{18... | collective-permute-start | bytes 6291464 | tf_op jit(solution)/shard_map/ppermute | solution.py:10
  50.4 38.1 %copy-start.7 = (bf16[1,768,2048]{2,1,0:T(8,128)(2,1)S(1)}, bf16[1,768,2048]{2,1,0:T(8,128)(2,1)}, u32[]{:S(2)}) copy-start(bf16[1,768,2048]{2,1,0:T(8,128)(2,1)} %param.19) | copy-start | bytes 9437188
  93.9 73.0 %reduce-scatter.6.cloned.1.call-start = ((), (), s32[]{:S(2)}) async-start(), calls=%async_computation.4 | async-start | bytes 4718592 | tf_op jit(solution)/shard_map/reduce_scatter | solution.py:108
  102.8 64.0 %reduce-scatter.8.cloned.1.call-start = ((), (), s32[]{:S(2)}) async-start(), calls=%async_computation.6 | async-start | bytes 4718592 | tf_op jit(solution)/shard_map/reduce_scatter | solution.py:109
  102.9 51.3 %collective-permute-start.3 = (bf16[512,2048]{1,0:T(8,128)(2,1)}, bf16[512,2048]{1,0:T(8,128)(2,1)}, u32[]{:S(2)}, u32[]{:S(2)}) collective-permute-start(bf16[512,2048]{1,0:T(8,128)(2,1)} %get-tuple-element.24), channel_id=1, source_target_pairs={{0,2},{2,4},{4,6},{6,8},{8,10},{10,12},{12,14},{14,16},{16,18},{18... | collective-permute-start | bytes 6291464 | tf_op jit(solution)/shard_map/ppermute | solution.py:10
  110.3 43.9 %copy-start.9 = (bf16[1,768,2048]{2,1,0:T(8,128)(2,1)S(1)}, bf16[1,768,2048]{2,1,0:T(8,128)(2,1)}, u32[]{:S(2)}) copy-start(bf16[1,768,2048]{2,1,0:T(8,128)(2,1)} %param.21) | copy-start | bytes 9437188
  159.5 22.9 %all-gather.8.cloned.1.call-start = ((), (), s32[]{:S(2)}) async-start(), calls=%async_computation.8 | async-start | bytes 2359296 | tf_op jit(solution)/shard_map/all_gather | solution.py:116
  159.5 7.2 %collective-permute-start = (bf16[512]{0:T(512)(128)(2,1)S(1)}, bf16[512]{0:T(512)(128)(2,1)S(1)}, u32[]{:S(2)}, u32[]{:S(2)}) collective-permute-start(bf16[512]{0:T(512)(128)(2,1)S(1)} %get-tuple-element.13), channel_id=1, source_target_pairs={{0,2},{2,4},{4,6},{6,8},{8,10},{10,12},{12,14},{14,16},{16,18},{18... | collective-permute-start | bytes 3080 | tf_op jit(solution)/shard_map/ppermute | solution.py:10
  171.6 23.7 %all-gather.6.cloned.1.call-start = ((), (), s32[]{:S(2)}) async-start(), calls=%async_computation.7 | async-start | bytes 2359296 | tf_op jit(solution)/shard_map/all_gather | solution.py:115
  172.1 36.1 %all-gather.4.cloned.1.call-start = ((), (), s32[]{:S(2)}) async-start(), calls=%async_computation.5 | async-start | bytes 2359296 | tf_op jit(solution)/shard_map/all_gather | solution.py:114
  201.8 91.8 %collective-permute-start.4 = (bf16[512,2048]{1,0:T(8,128)(2,1)}, bf16[512,2048]{1,0:T(8,128)(2,1)}, u32[]{:S(2)}, u32[]{:S(2)}) collective-permute-start(bf16[512,2048]{1,0:T(8,128)(2,1)} %add_convert_fusion.3), channel_id=1, source_target_pairs={{0,30},{2,0},{4,2},{6,4},{8,6},{10,8},{12,10},{14,12},{16,14},{18,... | collective-permute-start | bytes 6291464 | tf_op jit(solution)/shard_map/ppermute | solution.py:10
  208.2 11.1 %copy-start.11 = (bf16[2,512,768]{2,1,0:T(8,128)(2,1)S(1)}, bf16[2,512,768]{2,1,0:T(8,128)(2,1)}, u32[]{:S(2)}) copy-start(bf16[2,512,768]{2,1,0:T(8,128)(2,1)} %all-gather.8.cloned.1.call-done) | copy-start | bytes 4718596
  213.6 10.9 %copy-start.5 = (bf16[512,2048]{1,0:T(8,128)(2,1)S(1)}, bf16[512,2048]{1,0:T(8,128)(2,1)}, u32[]{:S(2)}) copy-start(bf16[512,2048]{1,0:T(8,128)(2,1)} %gather_fusion.2) | copy-start | bytes 6291460
  213.6 96.4 %collective-permute-start.2 = (bf16[512,2048]{1,0:T(8,128)(2,1)}, bf16[512,2048]{1,0:T(8,128)(2,1)}, u32[]{:S(2)}, u32[]{:S(2)}) collective-permute-start(bf16[512,2048]{1,0:T(8,128)(2,1)} %fusion.33), channel_id=1, source_target_pairs={{0,30},{2,0},{4,2},{6,4},{8,6},{10,8},{12,10},{14,12},{16,14},{18,... | collective-permute-start | bytes 6291464 | tf_op jit(solution)/shard_map/ppermute | solution.py:10
  224.5 3.6 %copy-start.13 = (bf16[2,512,768]{2,1,0:T(8,128)(2,1)S(1)}, bf16[2,512,768]{2,1,0:T(8,128)(2,1)}, u32[]{:S(2)}) copy-start(bf16[2,512,768]{2,1,0:T(8,128)(2,1)} %all-gather.4.cloned.1.call-done) | copy-start | bytes 4718596
  228.0 5.2 %copy-start.6 = (bf16[512,2048]{1,0:T(8,128)(2,1)S(1)}, bf16[512,2048]{1,0:T(8,128)(2,1)}, u32[]{:S(2)}) copy-start(bf16[512,2048]{1,0:T(8,128)(2,1)} %gather_fusion.4) | copy-start | bytes 6291460
  233.3 3.6 %copy-start.12 = (bf16[2,512,768]{2,1,0:T(8,128)(2,1)S(1)}, bf16[2,512,768]{2,1,0:T(8,128)(2,1)}, u32[]{:S(2)}) copy-start(bf16[2,512,768]{2,1,0:T(8,128)(2,1)} %all-gather.6.cloned.1.call-done) | copy-start | bytes 4718596
  240.5 3.8 %copy-start.8 = (bf16[1,768,2048]{2,1,0:T(8,128)(2,1)S(1)}, bf16[1,768,2048]{2,1,0:T(8,128)(2,1)}, u32[]{:S(2)}) copy-start(bf16[1,768,2048]{2,1,0:T(8,128)(2,1)} %param.19) | copy-start | bytes 9437188
  244.2 3.8 %copy-start.10 = (bf16[1,768,2048]{2,1,0:T(8,128)(2,1)S(1)}, bf16[1,768,2048]{2,1,0:T(8,128)(2,1)}, u32[]{:S(2)}) copy-start(bf16[1,768,2048]{2,1,0:T(8,128)(2,1)} %param.21) | copy-start | bytes 9437188
  280.5 6.3 %copy-start.1 = (bf16[768,2048]{1,0:T(8,128)(2,1)S(1)}, bf16[768,2048]{1,0:T(8,128)(2,1)}, u32[]{:S(2)}) copy-start(bf16[768,2048]{1,0:T(8,128)(2,1)} %convolution_convert_fusion) | copy-start | bytes 9437188
  280.5 6.3 %copy-start.2 = (bf16[768,2048]{1,0:T(8,128)(2,1)S(1)}, bf16[768,2048]{1,0:T(8,128)(2,1)}, u32[]{:S(2)}) copy-start(bf16[768,2048]{1,0:T(8,128)(2,1)} %convolution_convert_fusion.1) | copy-start | bytes 9437188
  286.7 3.1 copy-start.3
  286.7 3.8 %copy-start.4 = (bf16[768,2048]{1,0:T(8,128)(2,1)S(1)}, bf16[768,2048]{1,0:T(8,128)(2,1)}, u32[]{:S(2)}) copy-start(bf16[768,2048]{1,0:T(8,128)(2,1)} %convolution_convert_fusion.4) | copy-start | bytes 9437188
Sparse Core Ops, SparseCore 0:
  94.0 8.4 reduce-scatter.3
  105.3 12.2 reduce-scatter.5
  159.6 6.8 reduce-scatter.7
  171.7 10.6 all-gather.7
  184.3 10.9 all-gather.5
  197.3 10.9 all-gather.3
where the time goes:
time: 339 us; the launch traced here: 333 us
  waiting for transfers between devices  99.6 us (29%)
  other arithmetic  88.4 us (26%)
  matrix products  77.7 us (23%)
  local copies, waits for them, and re-layouts  37.1 us (11%)
  between operations  15.5 us (5%)
  starting transfers between devices  14.9 us (4%)
    ppermute x5, waiting for transfers between devices, passed_along(): return lax.ppermute(value, axis, pairs)  79.7 us
    gather x4, local copies, waits for them, and re-layouts, take_rows(): return jnp.take(array, index, axis=0, mode='fill', fill_value=0)  28.4 us
    scatter-add x2, other arithmetic, per_device(): empty.at[own_index].add(own_in, mode='drop').at[next_index]  25.1 us
    scatter-add x2, other arithmetic, per_device(): empty.at[own_index].add(own_out, mode='drop').at[next_index]  23 us
    ppermute x5, starting transfers between devices, passed_along(): return lax.ppermute(value, axis, pairs)  14.7 us
    dot_general x2, matrix products, finish_set(): in_rows = jnp.dot(grad_gate, wg, preferred_element_type=jnp.float32)  10.3 us
    all_gather x1, waiting for transfers between devices, per_device(): lax.all_gather(grad_up, 'dp', axis=2, tiled=True)  9.61 us
    dot_general x2, matrix products, finish_set(): out_rows = jnp.dot(scaled, wd, preferred_element_type=jnp.float32)  9.12 us
  transfers between devices with their start and end apart: 11, of which 6 were waited for; matrix products, arithmetic and copies ran while one was open for 45% of the time, Pallas kernels for 0%

commit v1 on v0

v1 whole, which is shorter than its diff:
```python
import jax
import jax.numpy as jnp
from jax import lax
from jax.sharding import PartitionSpec as P


def passed_along(value, axis, steps):
    count = lax.axis_size(axis)
    pairs = [(source, (source + steps) % count) for source in range(count)]
    return lax.ppermute(value, axis, pairs)


def route_weight(route_ids, weights_in, expert):
    hit = route_ids == expert
    return jnp.sum(jnp.where(hit, weights_in.astype(jnp.float32), 0.0), axis=1)


def slot_rows(route_ids, expert, capacity):
    count = route_ids.shape[0]
    member = jnp.any(route_ids == expert, axis=1)
    rank = jnp.cumsum(member.astype(jnp.int32), dtype=jnp.int32) - 1
    entries = jnp.arange(capacity, dtype=jnp.int32)
    chosen = member[None, :] & (rank[None, :] == entries[:, None])
    positions = jnp.arange(count, dtype=jnp.int32)
    index = jnp.sum(jnp.where(chosen, positions[None, :], 0), axis=1, dtype=jnp.int32)
    return jnp.where(jnp.any(chosen, axis=1), index, count)


def take_rows(array, index):
    if index is None:
        return array
    return jnp.take(array, index, axis=0, mode="fill", fill_value=0)


def add_rows(own, own_index, far, far_index, count):
    if own_index is None:
        return own + far
    empty = jnp.zeros((count, own.shape[1]), jnp.float32)
    return empty.at[own_index].add(own, mode="drop").at[far_index].add(far, mode="drop")


def summed_over_dp(part):
    if lax.axis_size("dp") == 2:
        return part + passed_along(part, "dp", 1)
    part = lax.psum_scatter(part, "dp", scatter_dimension=1, tiled=True)
    return lax.all_gather(part, "dp", axis=1, tiled=True)


def rows_by_weights(rows, weight):
    return lax.dot_general(rows, weight, (((1,), (1,)), ((), ())), preferred_element_type=jnp.float32)


def hidden_by_weights(hidden, weight):
    return jnp.dot(hidden, weight, preferred_element_type=jnp.float32)


def over_rows(hidden, rows):
    term = lax.dot_general(hidden, rows, (((0,), (0,)), ((), ())), preferred_element_type=jnp.float32)
    return term.astype(jnp.bfloat16)


def act_of(gate_val, up_val, weight_col):
    return (weight_col * (gate_val * jax.nn.sigmoid(gate_val)) * up_val).astype(jnp.bfloat16)


def slopes_of(gate_val, up_val, back_val, weight_col):
    sigmoid_val = jax.nn.sigmoid(gate_val)
    weighted = back_val * weight_col
    grad_gate = weighted * up_val * (sigmoid_val * (1.0 + gate_val * (1.0 - sigmoid_val)))
    grad_up = weighted * (gate_val * sigmoid_val)
    return grad_gate.astype(jnp.bfloat16), grad_up.astype(jnp.bfloat16)


def per_device(tokens, cotangent, routes, probs, expert_slot, pull_flags, w_gate, w_up, w_down):
    columns = lax.axis_size("expert")
    column = lax.axis_index("expert")
    count = tokens.shape[0]
    capacity = min(count, count * routes.shape[1] * 2 // columns)
    labels = jnp.arange(columns, dtype=jnp.int32)
    following = (column + 1) % columns
    wg, wu, wd = w_gate[0], w_up[0], w_down[0]

    def owner_expert(slot):
        return jnp.sum(jnp.where(expert_slot == slot, labels, 0), dtype=jnp.int32)

    flag = pull_flags[column].astype(jnp.float32)
    own_expert, next_expert = owner_expert(column), owner_expert(following)
    own_weight = route_weight(routes, probs, own_expert)
    next_weight = route_weight(routes, probs, next_expert) * flag
    own_index = next_index = None
    if capacity < count:
        own_index = slot_rows(routes, own_expert, capacity)
        next_index = slot_rows(routes, next_expert, capacity)
        own_weight = jnp.take(own_weight, own_index, mode="fill", fill_value=0.0)
        next_weight = jnp.take(next_weight, next_index, mode="fill", fill_value=0.0)
    own_x, own_dy = take_rows(tokens, own_index), take_rows(cotangent, own_index)
    far_x = passed_along(take_rows(tokens, next_index), "expert", 1)
    far_w = passed_along(next_weight.astype(jnp.bfloat16), "expert", 1)
    far_dy = passed_along(take_rows(cotangent, next_index), "expert", 1)
    own_w, far_w = own_weight[:, None], far_w.astype(jnp.float32)[:, None]

    own_gate = rows_by_weights(own_x, wg)
    own_gate = summed_over_dp(own_gate)
    own_up = summed_over_dp(rows_by_weights(own_x, wu))
    own_back = summed_over_dp(rows_by_weights(own_dy, wd))
    own_act = act_of(own_gate, own_up, own_w)
    own_dgate, own_dup = slopes_of(own_gate, own_up, own_back, own_w)
    own_out = hidden_by_weights(own_act, wd)
    own_in = hidden_by_weights(own_dgate, wg) + hidden_by_weights(own_dup, wu)
    own_out, own_in = lax.optimization_barrier((own_out, own_in))
    own_grads = (over_rows(own_dgate, own_x), over_rows(own_dup, own_x), over_rows(own_act, own_dy))
    own_grads = lax.optimization_barrier(own_grads)

    far_gate = summed_over_dp(rows_by_weights(far_x, wg))
    far_up = summed_over_dp(rows_by_weights(far_x, wu))
    far_act = act_of(far_gate, far_up, far_w)
    far_out = hidden_by_weights(far_act, wd).astype(jnp.bfloat16)
    next_out = passed_along(far_out, "expert", -1)

    far_dy, far_out = lax.optimization_barrier((far_dy, far_out))
    far_back = rows_by_weights(far_dy, wd)
    far_back = summed_over_dp(far_back)
    far_dgate, far_dup = slopes_of(far_gate, far_up, far_back, far_w)
    far_in = hidden_by_weights(far_dgate, wg) + hidden_by_weights(far_dup, wu)
    next_in = passed_along(far_in.astype(jnp.bfloat16), "expert", -1)

    far_grads = (over_rows(far_dgate, far_x), over_rows(far_dup, far_x), over_rows(far_act, far_dy))
    grad_sums = [
        (mine.astype(jnp.float32) + theirs.astype(jnp.float32)).astype(jnp.bfloat16)[None]
        for mine, theirs in zip(own_grads, far_grads)
    ]
    out_rows = add_rows(own_out, own_index, next_out.astype(jnp.float32), next_index, count)
    in_rows = add_rows(own_in, own_index, next_in.astype(jnp.float32), next_index, count)
    return (out_rows.astype(jnp.bfloat16), in_rows.astype(jnp.bfloat16), *grad_sums)


def solution(mesh):
    return jax.shard_map(
        per_device,
        mesh=mesh,
        in_specs=(
            P("expert", "dp"),
            P("expert", "dp"),
            P("expert", None),
            P("expert", None),
            P(),
            P(),
            P("expert", None, "dp"),
            P("expert", None, "dp"),
            P("expert", None, "dp"),
        ),
        out_specs=(
            P("expert", "dp"),
            P("expert", "dp"),
            P("expert", None, "dp"),
            P("expert", None, "dp"),
            P("expert", None, "dp"),
        ),
        check_vma=False,
    )
```

time: 339 us -> 220 us (0.65); the launches traced: 333 us -> 220 us
  other arithmetic: 88.4 us -> 12.9 us
  waiting for transfers between devices: 99.6 us -> 141 us
  local copies, waits for them, and re-layouts: 37.1 us -> 0.81 us
  matrix products: 77.7 us -> 57 us
  between operations: 15.5 us -> 1.56 us
  starting transfers between devices: 14.9 us -> 6.67 us
    ppermute x5 -> x11, waiting for transfers between devices: 79.7 us -> 141 us  [passed_along(): return lax.ppermute(value, axis, pairs)]
    scatter-add x4 -> x0, other arithmetic: 48 us -> none  [the longest x2 25.1 us: per_device(): empty.at[own_index].add(own_in, mode='drop').at[next_index]]
    gather x6 -> x0, local copies, waits for them, and re-layouts: 35.4 us -> none  [the longest x4 28.4 us: take_rows(): return jnp.take(array, index, axis=0, mode='fill', fill_value=0)]
    dot_general x18, matrix products: 77.7 us -> 57 us  [the longest x6 24.6 us: over_rows(): lax.dot_general(hidden, rows, (((0,), (0,)), ((), ())), preferred_element...]
    all_gather x3 -> x0, waiting for transfers between devices: 18.7 us -> none  [the longest x1 9.61 us: per_device(): lax.all_gather(grad_up, 'dp', axis=2, tiled=True)]
    broadcast_in_dim x3 -> x0, other arithmetic: 12.4 us -> none  [the longest x1 6.24 us: per_device(): grad_sums[1][None]]
    ppermute x5 -> x11, starting transfers between devices: 14.7 us -> 6.67 us  [passed_along(): return lax.ppermute(value, axis, pairs)]
    another operation x9 -> x0, other arithmetic: 6.3 us -> none  [the longest x1 1.87 us: per_device(): jnp.stack([lax.dot_general(one[0], one[3], contract, preferred_element_ty...]
  transfers between devices with their start and end apart: 11 -> 11, of which waited for: 6 -> 4; matrix products, arithmetic and copies ran while one was open for 45% -> 30% of each run, Pallas kernels for 0% -> 0%
where the time goes in v1:
time: 220 us
  waiting for transfers between devices  141 us (64%)
  matrix products  57 us (26%)
  other arithmetic  12.9 us (6%)
  starting transfers between devices  6.67 us (3%)
    ppermute x11, waiting for transfers between devices, passed_along(): return lax.ppermute(value, axis, pairs)  141 us
    dot_general x6, matrix products, over_rows(): lax.dot_general(hidden, rows, (((0,), (0,)), ((), ())), preferred_element...  24.6 us
    dot_general x6, matrix products, rows_by_weights(): lax.dot_general(rows, weight, (((1,), (1,)), ((), ())), preferred_element...  21.3 us
    dot_general x6, matrix products, hidden_by_weights(): return jnp.dot(hidden, weight, preferred_element_type=jnp.float32)  11.1 us
    ppermute x11, starting transfers between devices, passed_along(): return lax.ppermute(value, axis, pairs)  6.67 us
    convert_element_type x2, other arithmetic, slopes_of(): return (grad_gate.astype(jnp.bfloat16), grad_up.astype(jnp.bfloat16))  6.01 us
  transfers between devices with their start and end apart: 11, of which 4 were waited for; matrix products, arithmetic and copies ran while one was open for 30% of the time, Pallas kernels for 0%

profile of v1, /device:TPU:0, one launch (start us, length us, event | category | flops | bytes accessed | tf_op | source)
XLA Modules:
  0.0 220.1 jit_solution(7179383028326321739)
XLA Ops:
  0.6 0.0 copy-start
  0.6 0.0 copy-start.8
  0.7 3.0 %collective-permute-start.4 = (bf16[512,2048]{1,0:T(8,128)(2,1)}, bf16[512,2048]{1,0:T(8,128)(2,1)}, u32[]{:S(2)}, u32[]{:S(2)}) collective-permute-start(bf16[512,2048]{1,0:T(8,128)(2,1)} %param.9), channel_id=1, source_target_pairs={{0,2},{2,4},{4,6},{6,8},{8,10},{10,12},{12,14},{14,16},{16,18},{18... | collective-permute-start | bytes 6291464 | tf_op jit(solution)/shard_map/ppermute | solution.py:10
  3.7 5.5 %fusion.17 = f32[512,768]{1,0:T(8,128)} fusion(bf16[512,2048]{1,0:T(8,128)(2,1)} %param.9, bf16[1,768,2048]{2,1,0:T(8,128)(2,1)} %param.16), kind=kOutput, calls=%fused_computation.29 | convolution fusion | flops 1610612736 | bytes 6815744 | tf_op jit(solution)/shard_map/dot_general | solution.py:50
  9.2 3.0 %fusion.25 = f32[512,768]{1,0:T(8,128)} fusion(bf16[512,2048]{1,0:T(8,128)(2,1)S(1)} %copy-done.8, bf16[1,768,2048]{2,1,0:T(8,128)(2,1)S(1)} %copy-done.2), kind=kOutput, calls=%fused_computation.37 | convolution fusion | flops 1610612736 | bytes 6815744 | tf_op jit(solution)/shard_map/dot_general | solution.py:50
  12.2 0.6 collective-permute-start
  12.8 3.1 %fusion.7 = f32[512,768]{1,0:T(8,128)} fusion(bf16[512,2048]{1,0:T(8,128)(2,1)S(1)} %copy-done.10, bf16[1,768,2048]{2,1,0:T(8,128)(2,1)S(1)} %copy-done), kind=kOutput, calls=%fused_computation.19 | convolution fusion | flops 1610612736 | bytes 6815744 | tf_op jit(solution)/shard_map/dot_general | solution.py:50
  15.8 0.0 collective-permute-start.2
  15.9 0.6 dynamic_slice.3
  17.1 0.6 fusion.40
  17.8 1.3 fusion.38
  19.1 1.7 collective-permute-start.3
  20.8 32.8 %collective-permute-done.4 = bf16[512,2048]{1,0:T(8,128)(2,1)} collective-permute-done((bf16[512,2048]{1,0:T(8,128)(2,1)}, bf16[512,2048]{1,0:T(8,128)(2,1)}, u32[]{:S(2)}, u32[]{:S(2)}) %collective-permute-start.4) | collective-permute-done | bytes 2097184 | tf_op jit(solution)/shard_map/ppermute | solution.py:10
  53.6 4.3 %fusion.13 = f32[512,768]{1,0:T(8,128)S(1)} fusion(bf16[512,2048]{1,0:T(8,128)(2,1)} %collective-permute-done.4, bf16[1,768,2048]{2,1,0:T(8,128)(2,1)} %param.16), kind=kOutput, calls=%fused_computation.25 | convolution fusion | flops 1610612736 | bytes 6815744 | tf_op jit(solution)/shard_map/dot_general | solution.py:50
  58.0 0.0 copy-start.11
  58.0 0.1 collective-permute-start.6
  58.1 3.6 %fusion.21 = f32[512,768]{1,0:T(8,128)S(1)} fusion(bf16[512,2048]{1,0:T(8,128)(2,1)} %collective-permute-done.4, bf16[1,768,2048]{2,1,0:T(8,128)(2,1)S(1)} %copy-done.3), kind=kOutput, calls=%fused_computation.33 | convolution fusion | flops 1610612736 | bytes 6815744 | tf_op jit(solution)/shard_map/dot_general | solution.py:50
  61.7 0.4 collective-permute-start.5
  62.1 0.2 collective-permute-start.8
  62.4 0.0 copy-start.9
  62.4 4.9 %multiply_convert_fusion.4 = (bf16[512,768]{1,0:T(8,128)(2,1)S(1)}, bf16[512,768]{1,0:T(8,128)(2,1)S(1)}, bf16[512,768]{1,0:T(8,128)(2,1)S(1)}) fusion(f32[512,768]{1,0:T(8,128)} %fusion.17, f32[512,768]{1,0:T(8,128)} %collective-permute-done.1, f32[512,768]{1,0:T(8,128)} %fusion.25, f32[512,768]{1,0:T(8,128)} %collective-permute-done, ...), kind=kLoop, calls=%fused_computation.48 | loop fusion | flops 7864320 | bytes 11798528 | tf_op jit(solution)/shard_map/convert_element_type | solution.py:71
  67.3 3.5 %convolution_convert_fusion.5 = bf16[768,2048]{1,0:T(8,128)(2,1)} fusion(bf16[512,768]{1,0:T(8,128)(2,1)S(1)} %get-tuple-element.25, bf16[512,2048]{1,0:T(8,128)(2,1)S(1)} %copy-done.9), kind=kOutput, calls=%fused_computation.11 | convolution fusion | flops 1612185600 | bytes 6029312 | tf_op jit(solution)/shard_map/dot_general | solution.py:58
  70.9 3.5 %convolution_convert_fusion.4 = bf16[768,2048]{1,0:T(8,128)(2,1)} fusion(bf16[512,768]{1,0:T(8,128)(2,1)S(1)} %get-tuple-element.26, bf16[512,2048]{1,0:T(8,128)(2,1)S(1)} %copy-done.9), kind=kOutput, calls=%fused_computation.10 | convolution fusion | flops 1612185600 | bytes 6029312 | tf_op jit(solution)/shard_map/dot_general | solution.py:58
  74.4 0.7 multiply_convert_fusion.2
  75.1 1.8 fusion.30
  76.9 36.7 %collective-permute-done.8 = bf16[512,2048]{1,0:T(8,128)(2,1)S(1)} collective-permute-done((bf16[512,2048]{1,0:T(8,128)(2,1)S(1)}, bf16[512,2048]{1,0:T(8,128)(2,1)S(1)}, u32[]{:S(2)}, u32[]{:S(2)}) %collective-permute-start.8) | collective-permute-done | bytes 2097184 | tf_op jit(solution)/shard_map/ppermute | solution.py:10
  113.6 1.8 fusion.3
  115.5 0.1 collective-permute-start.9
  115.5 3.5 %convolution_convert_fusion.3 = bf16[768,2048]{1,0:T(8,128)(2,1)} fusion(bf16[512,768]{1,0:T(8,128)(2,1)S(1)} %get-tuple-element.27, bf16[512,2048]{1,0:T(8,128)(2,1)S(1)} %copy-done.11), kind=kOutput, calls=%fused_computation.9 | convolution fusion | flops 1612185600 | bytes 6029312 | tf_op jit(solution)/shard_map/dot_general | solution.py:58
  119.1 1.8 fusion.9
  120.9 0.1 copy-done.7
  120.9 1.8 fusion.15
  122.8 2.1 fusion.27
  124.8 0.1 collective-permute-start.7
  124.9 1.1 multiply_convert_fusion.1
  126.0 1.8 fusion.11
  127.8 0.0 copy-start.15
  127.8 1.8 add_convert_fusion.4
  129.7 0.0 copy-start.14
  129.7 0.5 collective-permute-start.10
  130.2 3.6 %fusion.2 = bf16[1,768,2048]{2,1,0:T(8,128)(2,1)} fusion(bf16[768,2048]{1,0:T(8,128)(2,1)S(1)} %copy-done.15, bf16[512,768]{1,0:T(8,128)(2,1)S(1)} %get-tuple-element.21, bf16[512,2048]{1,0:T(8,128)(2,1)S(1)} %collective-permute-done.8), kind=kOutput, calls=%fused_computation.14 | convolution fusion | flops 1618477056 | bytes 9175040 | tf_op jit(solution)/shard_map/dot_general | solution.py:58
  133.8 5.2 %fusion = bf16[1,768,2048]{2,1,0:T(8,128)(2,1)} fusion(bf16[768,2048]{1,0:T(8,128)(2,1)S(1)} %copy-done.14, bf16[512,768]{1,0:T(8,128)(2,1)S(1)} %get-tuple-element.23, bf16[512,2048]{1,0:T(8,128)(2,1)} %collective-permute-done.4), kind=kOutput, calls=%fused_computation.12 | convolution fusion | flops 1618477056 | bytes 9175040 | tf_op jit(solution)/shard_map/dot_general | solution.py:58
  139.0 5.2 %fusion.1 = bf16[1,768,2048]{2,1,0:T(8,128)(2,1)} fusion(bf16[768,2048]{1,0:T(8,128)(2,1)S(1)} %copy-done.13, bf16[512,768]{1,0:T(8,128)(2,1)S(1)} %get-tuple-element.24, bf16[512,2048]{1,0:T(8,128)(2,1)} %collective-permute-done.4), kind=kOutput, calls=%fused_computation.13 | convolution fusion | flops 1618477056 | bytes 9175040 | tf_op jit(solution)/shard_map/dot_general | solution.py:58
  144.2 29.2 %collective-permute-done.7 = bf16[512,2048]{1,0:T(8,128)(2,1)S(1)} collective-permute-done((bf16[512,2048]{1,0:T(8,128)(2,1)S(1)}, bf16[512,2048]{1,0:T(8,128)(2,1)S(1)}, u32[]{:S(2)}, u32[]{:S(2)}) %collective-permute-start.7) | collective-permute-done | bytes 2097184 | tf_op jit(solution)/shard_map/ppermute | solution.py:10
  173.4 2.1 add_convert_fusion.5
  175.5 42.3 %collective-permute-done.10 = bf16[512,2048]{1,0:T(8,128)(2,1)S(1)} collective-permute-done((bf16[512,2048]{1,0:T(8,128)(2,1)S(1)}, bf16[512,2048]{1,0:T(8,128)(2,1)S(1)}, u32[]{:S(2)}, u32[]{:S(2)}) %collective-permute-start.10) | collective-permute-done | bytes 2097184 | tf_op jit(solution)/shard_map/ppermute | solution.py:10
  217.9 2.1 add_convert_fusion.3
  220.0 0.1 copy-done.1
  (34 shorter events, 0.1 us)
Async XLA Ops:
  0.6 12.1 %copy-start = (bf16[1,768,2048]{2,1,0:T(8,128)(2,1)S(1)}, bf16[1,768,2048]{2,1,0:T(8,128)(2,1)}, u32[]{:S(2)}) copy-start(bf16[1,768,2048]{2,1,0:T(8,128)(2,1)} %param.17) | copy-start | bytes 9437188
  0.6 8.5 %copy-start.8 = (bf16[512,2048]{1,0:T(8,128)(2,1)S(1)}, bf16[512,2048]{1,0:T(8,128)(2,1)}, u32[]{:S(2)}) copy-start(bf16[512,2048]{1,0:T(8,128)(2,1)} %param.9) | copy-start | bytes 6291460
  0.7 8.5 %copy-start.2 = (bf16[1,768,2048]{2,1,0:T(8,128)(2,1)S(1)}, bf16[1,768,2048]{2,1,0:T(8,128)(2,1)}, u32[]{:S(2)}) copy-start(bf16[1,768,2048]{2,1,0:T(8,128)(2,1)} %param.15) | copy-start | bytes 9437188
  0.7 53.0 %collective-permute-start.4 = (bf16[512,2048]{1,0:T(8,128)(2,1)}, bf16[512,2048]{1,0:T(8,128)(2,1)}, u32[]{:S(2)}, u32[]{:S(2)}) collective-permute-start(bf16[512,2048]{1,0:T(8,128)(2,1)} %param.9), channel_id=1, source_target_pairs={{0,2},{2,4},{4,6},{6,8},{8,10},{10,12},{12,14},{14,16},{16,18},{18... | collective-permute-start | bytes 6291464 | tf_op jit(solution)/shard_map/ppermute | solution.py:10
  9.2 3.6 %copy-start.10 = (bf16[512,2048]{1,0:T(8,128)(2,1)S(1)}, bf16[512,2048]{1,0:T(8,128)(2,1)}, u32[]{:S(2)}) copy-start(bf16[512,2048]{1,0:T(8,128)(2,1)} %param.10) | copy-start | bytes 6291460
  9.2 52.9 %collective-permute-start.1 = (f32[512,768]{1,0:T(8,128)}, f32[512,768]{1,0:T(8,128)}, u32[]{:S(2)}, u32[]{:S(2)}) collective-permute-start(f32[512,768]{1,0:T(8,128)} %fusion.17), channel_id=1, source_target_pairs={{0,1},{1,0},{2,3},{3,2},{4,5},{5,4},{6,7},{7,6},{8,9},{9,8},{10,11... | collective-permute-start | bytes 4718600 | tf_op jit(solution)/shard_map/ppermute | solution.py:10
  12.2 3.7 %copy-start.12 = (s32[16]{0:T(128)S(1)}, s32[16]{0:T(128)}, u32[]{:S(2)}) copy-start(s32[16]{0:T(128)} %param.14) | copy-start | bytes 196
  12.2 4.9 %copy-start.6 = (s32[16]{0:T(128)S(1)}, s32[16]{0:T(128)}, u32[]{:S(2)}) copy-start(s32[16]{0:T(128)} %param.13) | copy-start | bytes 196
  12.2 5.6 %copy-start.4 = (s32[512,8]{0,1:T(8,128)S(1)}, s32[512,8]{0,1:T(8,128)}, u32[]{:S(2)}) copy-start(s32[512,8]{0,1:T(8,128)} %param.11) | copy-start | bytes 49156
  12.2 5.6 %copy-start.5 = (bf16[512,8]{0,1:T(8,128)(2,1)S(1)}, bf16[512,8]{0,1:T(8,128)(2,1)}, u32[]{:S(2)}) copy-start(bf16[512,8]{0,1:T(8,128)(2,1)} %param.12) | copy-start | bytes 24580
  12.2 50.2 %collective-permute-start = (f32[512,768]{1,0:T(8,128)}, f32[512,768]{1,0:T(8,128)}, u32[]{:S(2)}, u32[]{:S(2)}) collective-permute-start(f32[512,768]{1,0:T(8,128)} %fusion.25), channel_id=1, source_target_pairs={{0,1},{1,0},{2,3},{3,2},{4,5},{5,4},{6,7},{7,6},{8,9},{9,8},{10,11... | collective-permute-start | bytes 4718600 | tf_op jit(solution)/shard_map/ppermute | solution.py:10
  15.8 46.5 %collective-permute-start.2 = (f32[512,768]{1,0:T(8,128)}, f32[512,768]{1,0:T(8,128)}, u32[]{:S(2)}, u32[]{:S(2)}) collective-permute-start(f32[512,768]{1,0:T(8,128)} %fusion.7), channel_id=1, source_target_pairs={{0,1},{1,0},{2,3},{3,2},{4,5},{5,4},{6,7},{7,6},{8,9},{9,8},{10,11... | collective-permute-start | bytes 4718600 | tf_op jit(solution)/shard_map/ppermute | solution.py:10
  19.1 39.0 %copy-start.3 = (bf16[1,768,2048]{2,1,0:T(8,128)(2,1)S(1)}, bf16[1,768,2048]{2,1,0:T(8,128)(2,1)}, u32[]{:S(2)}) copy-start(bf16[1,768,2048]{2,1,0:T(8,128)(2,1)} %param.15) | copy-start | bytes 9437188
  19.1 42.6 %collective-permute-start.3 = (bf16[512]{0:T(512)(128)(2,1)S(1)}, bf16[512]{0:T(512)(128)(2,1)S(1)}, u32[]{:S(2)}, u32[]{:S(2)}) collective-permute-start(bf16[512]{0:T(512)(128)(2,1)S(1)} %multiply_convert_fusion.6), channel_id=1, source_target_pairs={{0,2},{2,4},{4,6},{6,8},{8,10},{10,12},{12,14},{14,16},{16,18},{18... | collective-permute-start | bytes 3080 | tf_op jit(solution)/shard_map/ppermute | solution.py:10
  58.0 4.1 %copy-start.11 = (bf16[512,2048]{1,0:T(8,128)(2,1)S(1)}, bf16[512,2048]{1,0:T(8,128)(2,1)}, u32[]{:S(2)}) copy-start(bf16[512,2048]{1,0:T(8,128)(2,1)} %param.10) | copy-start | bytes 6291460
  58.0 16.3 %collective-permute-start.6 = (f32[512,768]{1,0:T(8,128)S(1)}, f32[512,768]{1,0:T(8,128)S(1)}, u32[]{:S(2)}, u32[]{:S(2)}) collective-permute-start(f32[512,768]{1,0:T(8,128)S(1)} %fusion.13), channel_id=1, source_target_pairs={{0,1},{1,0},{2,3},{3,2},{4,5},{5,4},{6,7},{7,6},{8,9},{9,8},{10,11... | collective-permute-start | bytes 4718600 | tf_op jit(solution)/shard_map/ppermute | solution.py:10
  61.7 12.7 %collective-permute-start.5 = (f32[512,768]{1,0:T(8,128)S(1)}, f32[512,768]{1,0:T(8,128)S(1)}, u32[]{:S(2)}, u32[]{:S(2)}) collective-permute-start(f32[512,768]{1,0:T(8,128)S(1)} %fusion.21), channel_id=1, source_target_pairs={{0,1},{1,0},{2,3},{3,2},{4,5},{5,4},{6,7},{7,6},{8,9},{9,8},{10,11... | collective-permute-start | bytes 4718600 | tf_op jit(solution)/shard_map/ppermute | solution.py:10
  62.1 51.5 %collective-permute-start.8 = (bf16[512,2048]{1,0:T(8,128)(2,1)S(1)}, bf16[512,2048]{1,0:T(8,128)(2,1)S(1)}, u32[]{:S(2)}, u32[]{:S(2)}) collective-permute-start(bf16[512,2048]{1,0:T(8,128)(2,1)S(1)} %copy-done.11), channel_id=1, source_target_pairs={{0,2},{2,4},{4,6},{6,8},{8,10},{10,12},{12,14},{14,16},{16,18},{18... | collective-permute-start | bytes 6291464 | tf_op jit(solution)/shard_map/ppermute | solution.py:10
  62.4 4.9 %copy-start.9 = (bf16[512,2048]{1,0:T(8,128)(2,1)S(1)}, bf16[512,2048]{1,0:T(8,128)(2,1)}, u32[]{:S(2)}) copy-start(bf16[512,2048]{1,0:T(8,128)(2,1)} %param.9) | copy-start | bytes 6291460
  115.5 9.4 %collective-permute-start.9 = (f32[512,768]{1,0:T(8,128)S(1)}, f32[512,768]{1,0:T(8,128)S(1)}, u32[]{:S(2)}, u32[]{:S(2)}) collective-permute-start(f32[512,768]{1,0:T(8,128)S(1)} %fusion.3), channel_id=1, source_target_pairs={{0,1},{1,0},{2,3},{3,2},{4,5},{5,4},{6,7},{7,6},{8,9},{9,8},{10,11... | collective-permute-start | bytes 4718600 | tf_op jit(solution)/shard_map/ppermute | solution.py:10
  119.1 1.9 copy-start.7
  124.8 48.6 %collective-permute-start.7 = (bf16[512,2048]{1,0:T(8,128)(2,1)S(1)}, bf16[512,2048]{1,0:T(8,128)(2,1)S(1)}, u32[]{:S(2)}, u32[]{:S(2)}) collective-permute-start(bf16[512,2048]{1,0:T(8,128)(2,1)S(1)} %fusion.30), channel_id=1, source_target_pairs={{0,30},{2,0},{4,2},{6,4},{8,6},{10,8},{12,10},{14,12},{16,14},{18,... | collective-permute-start | bytes 6291464 | tf_op jit(solution)/shard_map/ppermute | solution.py:10
  127.8 2.4 %copy-start.15 = (bf16[768,2048]{1,0:T(8,128)(2,1)S(1)}, bf16[768,2048]{1,0:T(8,128)(2,1)}, u32[]{:S(2)}) copy-start(bf16[768,2048]{1,0:T(8,128)(2,1)} %convolution_convert_fusion.3) | copy-start | bytes 9437188
  129.7 4.1 %copy-start.14 = (bf16[768,2048]{1,0:T(8,128)(2,1)S(1)}, bf16[768,2048]{1,0:T(8,128)(2,1)}, u32[]{:S(2)}) copy-start(bf16[768,2048]{1,0:T(8,128)(2,1)} %convolution_convert_fusion.5) | copy-start | bytes 9437188
  129.7 88.2 %collective-permute-start.10 = (bf16[512,2048]{1,0:T(8,128)(2,1)S(1)}, bf16[512,2048]{1,0:T(8,128)(2,1)S(1)}, u32[]{:S(2)}, u32[]{:S(2)}) collective-permute-start(bf16[512,2048]{1,0:T(8,128)(2,1)S(1)} %add_convert_fusion.4), channel_id=1, source_target_pairs={{0,30},{2,0},{4,2},{6,4},{8,6},{10,8},{12,10},{14,12},{16,14},{18,... | collective-permute-start | bytes 6291464 | tf_op jit(solution)/shard_map/ppermute | solution.py:10
  133.8 5.2 %copy-start.13 = (bf16[768,2048]{1,0:T(8,128)(2,1)S(1)}, bf16[768,2048]{1,0:T(8,128)(2,1)}, u32[]{:S(2)}) copy-start(bf16[768,2048]{1,0:T(8,128)(2,1)} %convolution_convert_fusion.4) | copy-start | bytes 9437188
  217.9 2.2 copy-start.1

commit v2 on v1

--- a/solution.py
+++ b/solution.py
@@ -96,7 +96,11 @@
     own_x, own_dy = take_rows(tokens, own_index), take_rows(cotangent, own_index)
     far_x = passed_along(take_rows(tokens, next_index), "expert", 1)
     far_w = passed_along(next_weight.astype(jnp.bfloat16), "expert", 1)
-    far_dy = passed_along(take_rows(cotangent, next_index), "expert", 1)
+    next_dy = take_rows(cotangent, next_index)
+    dy_cut = capacity - capacity // 16
+    cut = capacity - capacity // 8
+    far_dy_head = passed_along(next_dy[:dy_cut], "expert", 1)
+    far_dy_tail = passed_along(next_dy[dy_cut:], "expert", 1)
     own_w, far_w = own_weight[:, None], far_w.astype(jnp.float32)[:, None]
 
     own_gate = rows_by_weights(own_x, wg)
@@ -117,12 +121,15 @@
     far_out = hidden_by_weights(far_act, wd).astype(jnp.bfloat16)
     next_out = passed_along(far_out, "expert", -1)
 
-    far_dy, far_out = lax.optimization_barrier((far_dy, far_out))
+    far_dy_head, far_dy_tail, far_out = lax.optimization_barrier((far_dy_head, far_dy_tail, far_out))
+    far_dy = jnp.concatenate([far_dy_head, far_dy_tail])
     far_back = rows_by_weights(far_dy, wd)
     far_back = summed_over_dp(far_back)
     far_dgate, far_dup = slopes_of(far_gate, far_up, far_back, far_w)
     far_in = hidden_by_weights(far_dgate, wg) + hidden_by_weights(far_dup, wu)
-    next_in = passed_along(far_in.astype(jnp.bfloat16), "expert", -1)
+    far_in = far_in.astype(jnp.bfloat16)
+    next_in_head = passed_along(far_in[:cut], "expert", -1)
+    next_in_tail = passed_along(far_in[cut:], "expert", -1)
 
     far_grads = (over_rows(far_dgate, far_x), over_rows(far_dup, far_x), over_rows(far_act, far_dy))
     grad_sums = [
@@ -130,8 +137,15 @@
         for mine, theirs in zip(own_grads, far_grads)
     ]
     out_rows = add_rows(own_out, own_index, next_out.astype(jnp.float32), next_index, count)
-    in_rows = add_rows(own_in, own_index, next_in.astype(jnp.float32), next_index, count)
-    return (out_rows.astype(jnp.bfloat16), in_rows.astype(jnp.bfloat16), *grad_sums)
+    if next_index is None:
+        head = own_in + jnp.pad(next_in_head, ((0, count - cut), (0, 0))).astype(jnp.float32)
+        head = lax.optimization_barrier(head.astype(jnp.bfloat16))
+        tail = (own_in[cut:] + next_in_tail.astype(jnp.float32)).astype(jnp.bfloat16)
+        in_rows = lax.dynamic_update_slice(head, tail, (cut, 0))
+    else:
+        next_in = jnp.concatenate([next_in_head, next_in_tail]).astype(jnp.float32)
+        in_rows = add_rows(own_in, own_index, next_in, next_index, count).astype(jnp.bfloat16)
+    return (out_rows.astype(jnp.bfloat16), in_rows, *grad_sums)
 
 
 def solution(mesh):

time: 220 us -> 220 us (level)
  waiting for transfers between devices: 141 us -> 138 us
  local copies, waits for them, and re-layouts: 0.81 us -> 3.76 us
    ppermute x11 -> x13, waiting for transfers between devices: 141 us -> 138 us  [passed_along(): return lax.ppermute(value, axis, pairs)]
    unnamed x32 -> x35, local copies, waits for them, and re-layouts: 0.22 us -> 2.72 us
    ppermute x11 -> x13, starting transfers between devices: 6.67 us -> 7.24 us  [passed_along(): return lax.ppermute(value, axis, pairs)]
  transfers between devices with their start and end apart: 11 -> 13, of which waited for: 4 -> 5; matrix products, arithmetic and copies ran while one was open for 30% -> 31% of each run, Pallas kernels for 0% -> 0%
where the time goes in v2:
time: 220 us; the launch traced here: 219 us
  waiting for transfers between devices  138 us (63%)
  matrix products  57 us (26%)
  other arithmetic  11.6 us (5%)
  starting transfers between devices  7.24 us (3%)
  local copies, waits for them, and re-layouts  3.76 us (2%)
    ppermute x13, waiting for transfers between devices, passed_along(): return lax.ppermute(value, axis, pairs)  138 us
    dot_general x6, matrix products, over_rows(): lax.dot_general(hidden, rows, (((0,), (0,)), ((), ())), preferred_element...  24.5 us
    dot_general x6, matrix products, rows_by_weights(): lax.dot_general(rows, weight, (((1,), (1,)), ((), ())), preferred_element...  21.3 us
    dot_general x6, matrix products, hidden_by_weights(): return jnp.dot(hidden, weight, preferred_element_type=jnp.float32)  11.2 us
    ppermute x13, starting transfers between devices, passed_along(): return lax.ppermute(value, axis, pairs)  7.24 us
    convert_element_type x2, other arithmetic, slopes_of(): return (grad_gate.astype(jnp.bfloat16), grad_up.astype(jnp.bfloat16))  6.01 us
  transfers between devices with their start and end apart: 13, of which 5 were waited for; matrix products, arithmetic and copies ran while one was open for 31% of the time, Pallas kernels for 0%

profile of v2, /device:TPU:0, one launch (start us, length us, event | category | flops | bytes accessed | tf_op | source)
XLA Modules:
  0.0 219.4 jit_solution(11382233408691707873)
XLA Ops:
  0.7 3.0 %collective-permute-start.4 = (bf16[512,2048]{1,0:T(8,128)(2,1)}, bf16[512,2048]{1,0:T(8,128)(2,1)}, u32[]{:S(2)}, u32[]{:S(2)}) collective-permute-start(bf16[512,2048]{1,0:T(8,128)(2,1)} %param.9), channel_id=1, source_target_pairs={{0,2},{2,4},{4,6},{6,8},{8,10},{10,12},{12,14},{14,16},{16,18},{18... | collective-permute-start | bytes 6291464 | tf_op jit(solution)/shard_map/ppermute | solution.py:10
  3.7 5.5 %fusion.17 = f32[512,768]{1,0:T(8,128)} fusion(bf16[512,2048]{1,0:T(8,128)(2,1)} %param.9, bf16[1,768,2048]{2,1,0:T(8,128)(2,1)} %param.16), kind=kOutput, calls=%fused_computation.29 | convolution fusion | flops 1610612736 | bytes 6815744 | tf_op jit(solution)/shard_map/dot_general | solution.py:50
  9.2 3.0 %fusion.25 = f32[512,768]{1,0:T(8,128)} fusion(bf16[512,2048]{1,0:T(8,128)(2,1)S(1)} %copy-done.11, bf16[1,768,2048]{2,1,0:T(8,128)(2,1)S(1)} %copy-done.2), kind=kOutput, calls=%fused_computation.37 | convolution fusion | flops 1610612736 | bytes 6815744 | tf_op jit(solution)/shard_map/dot_general | solution.py:50
  12.2 0.6 collective-permute-start
  12.8 3.1 %fusion.7 = f32[512,768]{1,0:T(8,128)} fusion(bf16[512,2048]{1,0:T(8,128)(2,1)S(1)} %copy-done.4, bf16[1,768,2048]{2,1,0:T(8,128)(2,1)S(1)} %copy-done), kind=kOutput, calls=%fused_computation.19 | convolution fusion | flops 1610612736 | bytes 6815744 | tf_op jit(solution)/shard_map/dot_general | solution.py:50
  15.9 0.6 dynamic_slice.3
  17.1 0.6 fusion.41
  17.8 1.3 fusion.39
  19.1 1.7 collective-permute-start.3
  20.8 32.8 %collective-permute-done.4 = bf16[512,2048]{1,0:T(8,128)(2,1)} collective-permute-done((bf16[512,2048]{1,0:T(8,128)(2,1)}, bf16[512,2048]{1,0:T(8,128)(2,1)}, u32[]{:S(2)}, u32[]{:S(2)}) %collective-permute-start.4) | collective-permute-done | bytes 2097184 | tf_op jit(solution)/shard_map/ppermute | solution.py:10
  53.6 4.3 %fusion.13 = f32[512,768]{1,0:T(8,128)S(1)} fusion(bf16[512,2048]{1,0:T(8,128)(2,1)} %collective-permute-done.4, bf16[1,768,2048]{2,1,0:T(8,128)(2,1)} %param.16), kind=kOutput, calls=%fused_computation.25 | convolution fusion | flops 1610612736 | bytes 6815744 | tf_op jit(solution)/shard_map/dot_general | solution.py:50
  58.0 0.1 collective-permute-start.6
  58.1 3.6 %fusion.21 = f32[512,768]{1,0:T(8,128)S(1)} fusion(bf16[512,2048]{1,0:T(8,128)(2,1)} %collective-permute-done.4, bf16[1,768,2048]{2,1,0:T(8,128)(2,1)S(1)} %copy-done.3), kind=kOutput, calls=%fused_computation.33 | convolution fusion | flops 1610612736 | bytes 6815744 | tf_op jit(solution)/shard_map/dot_general | solution.py:50
  61.7 0.4 collective-permute-start.5
  62.1 0.2 slice.15
  62.4 0.1 collective-permute-start.9
  62.4 0.2 collective-permute-start.8
  62.7 4.9 %multiply_convert_fusion.4 = (bf16[512,768]{1,0:T(8,128)(2,1)S(1)}, bf16[512,768]{1,0:T(8,128)(2,1)S(1)}, bf16[512,768]{1,0:T(8,128)(2,1)S(1)}) fusion(f32[512,768]{1,0:T(8,128)} %fusion.17, f32[512,768]{1,0:T(8,128)} %collective-permute-done.1, f32[512,768]{1,0:T(8,128)} %fusion.25, f32[512,768]{1,0:T(8,128)} %collective-permute-done, ...), kind=kLoop, calls=%fused_computation.48 | loop fusion | flops 7864320 | bytes 11798528 | tf_op jit(solution)/shard_map/convert_element_type | solution.py:71
  67.6 3.5 %convolution_convert_fusion.5 = bf16[768,2048]{1,0:T(8,128)(2,1)} fusion(bf16[512,768]{1,0:T(8,128)(2,1)S(1)} %get-tuple-element.27, bf16[512,2048]{1,0:T(8,128)(2,1)S(1)} %copy-done.12), kind=kOutput, calls=%fused_computation.11 | convolution fusion | flops 1612185600 | bytes 6029312 | tf_op jit(solution)/shard_map/dot_general | solution.py:58
  71.2 3.5 %convolution_convert_fusion.4 = bf16[768,2048]{1,0:T(8,128)(2,1)} fusion(bf16[512,768]{1,0:T(8,128)(2,1)S(1)} %get-tuple-element.28, bf16[512,2048]{1,0:T(8,128)(2,1)S(1)} %copy-done.12), kind=kOutput, calls=%fused_computation.10 | convolution fusion | flops 1612185600 | bytes 6029312 | tf_op jit(solution)/shard_map/dot_general | solution.py:58
  74.6 0.7 multiply_convert_fusion.2
  75.4 1.8 fusion.30
  77.2 36.5 %collective-permute-done.8 = bf16[480,2048]{1,0:T(8,128)(2,1)S(1)} collective-permute-done((bf16[480,2048]{1,0:T(8,128)(2,1)S(1)}, bf16[480,2048]{1,0:T(8,128)(2,1)S(1)}, u32[]{:S(2)}, u32[]{:S(2)}) %collective-permute-start.8) | collective-permute-done | bytes 1966112 | tf_op jit(solution)/shard_map/ppermute | solution.py:10
  113.7 0.1 constant_dynamic-update-slice_fusion.1
  113.8 1.8 fusion.3
  115.7 0.1 collective-permute-start.10
  115.8 3.5 %convolution_convert_fusion.3 = bf16[768,2048]{1,0:T(8,128)(2,1)} fusion(bf16[512,768]{1,0:T(8,128)(2,1)S(1)} %get-tuple-element.29, bf16[512,2048]{1,0:T(8,128)(2,1)S(1)} %copy-done.5), kind=kOutput, calls=%fused_computation.9 | convolution fusion | flops 1612185600 | bytes 6029312 | tf_op jit(solution)/shard_map/dot_general | solution.py:58
  119.3 1.8 fusion.9
  121.2 1.8 fusion.15
  123.0 2.1 fusion.27
  125.0 0.1 collective-permute-start.7
  125.1 1.1 multiply_convert_fusion.1
  126.2 1.8 fusion.11
  128.0 1.8 add_convert_fusion.4
  129.9 0.2 slice.20
  130.1 0.5 collective-permute-start.11
  130.6 1.2 copy-done.16
  131.8 3.5 %fusion.2 = bf16[1,768,2048]{2,1,0:T(8,128)(2,1)} fusion(bf16[768,2048]{1,0:T(8,128)(2,1)S(1)} %copy-done.16, bf16[512,768]{1,0:T(8,128)(2,1)S(1)} %get-tuple-element.23, bf16[512,2048]{1,0:T(8,128)(2,1)S(1)} %constant_dynamic-update-slice_fusion), kind=kOutput, calls=%fused_computation.14 | convolution fusion | flops 1618477056 | bytes 9175040 | tf_op jit(solution)/shard_map/dot_general | solution.py:58
  135.3 0.5 collective-permute-start.12
  135.8 5.4 %fusion = bf16[1,768,2048]{2,1,0:T(8,128)(2,1)} fusion(bf16[768,2048]{1,0:T(8,128)(2,1)S(1)} %copy-done.15, bf16[512,768]{1,0:T(8,128)(2,1)S(1)} %get-tuple-element.25, bf16[512,2048]{1,0:T(8,128)(2,1)} %collective-permute-done.4), kind=kOutput, calls=%fused_computation.12 | convolution fusion | flops 1618477056 | bytes 9175040 | tf_op jit(solution)/shard_map/dot_general | solution.py:58
  141.2 5.1 %fusion.1 = bf16[1,768,2048]{2,1,0:T(8,128)(2,1)} fusion(bf16[768,2048]{1,0:T(8,128)(2,1)S(1)} %copy-done.14, bf16[512,768]{1,0:T(8,128)(2,1)S(1)} %get-tuple-element.26, bf16[512,2048]{1,0:T(8,128)(2,1)} %collective-permute-done.4), kind=kOutput, calls=%fused_computation.13 | convolution fusion | flops 1618477056 | bytes 9175040 | tf_op jit(solution)/shard_map/dot_general | solution.py:58
  146.3 27.3 %collective-permute-done.7 = bf16[512,2048]{1,0:T(8,128)(2,1)S(1)} collective-permute-done((bf16[512,2048]{1,0:T(8,128)(2,1)S(1)}, bf16[512,2048]{1,0:T(8,128)(2,1)S(1)}, u32[]{:S(2)}, u32[]{:S(2)}) %collective-permute-start.7) | collective-permute-done | bytes 2097184 | tf_op jit(solution)/shard_map/ppermute | solution.py:10
  173.6 2.1 add_convert_fusion.5
  175.7 37.2 %collective-permute-done.11 = bf16[448,2048]{1,0:T(8,128)(2,1)S(1)} collective-permute-done((bf16[448,2048]{1,0:T(8,128)(2,1)S(1)}, bf16[448,2048]{1,0:T(8,128)(2,1)S(1)}, u32[]{:S(2)}, u32[]{:S(2)}) %collective-permute-start.11) | collective-permute-done | bytes 1835040 | tf_op jit(solution)/shard_map/ppermute | solution.py:10
  212.9 0.7 add_convert_fusion.3
  213.6 4.4 %collective-permute-done.12 = bf16[64,2048]{1,0:T(8,128)(2,1)S(1)} collective-permute-done((bf16[64,2048]{1,0:T(8,128)(2,1)S(1)}, bf16[64,2048]{1,0:T(8,128)(2,1)S(1)}, u32[]{:S(2)}, u32[]{:S(2)}) %collective-permute-start.12) | collective-permute-done | bytes 262176 | tf_op jit(solution)/shard_map/ppermute | solution.py:10
  218.1 0.1 fusion.37
  218.1 1.3 copy-done.6
  (47 shorter events, 0.2 us)
Async XLA Ops:
  0.6 12.1 %copy-start = (bf16[1,768,2048]{2,1,0:T(8,128)(2,1)S(1)}, bf16[1,768,2048]{2,1,0:T(8,128)(2,1)}, u32[]{:S(2)}) copy-start(bf16[1,768,2048]{2,1,0:T(8,128)(2,1)} %param.17) | copy-start | bytes 9437188
  0.6 8.5 %copy-start.11 = (bf16[512,2048]{1,0:T(8,128)(2,1)S(1)}, bf16[512,2048]{1,0:T(8,128)(2,1)}, u32[]{:S(2)}) copy-start(bf16[512,2048]{1,0:T(8,128)(2,1)} %param.9) | copy-start | bytes 6291460
  0.7 8.5 %copy-start.2 = (bf16[1,768,2048]{2,1,0:T(8,128)(2,1)S(1)}, bf16[1,768,2048]{2,1,0:T(8,128)(2,1)}, u32[]{:S(2)}) copy-start(bf16[1,768,2048]{2,1,0:T(8,128)(2,1)} %param.15) | copy-start | bytes 9437188
  0.7 53.0 %collective-permute-start.4 = (bf16[512,2048]{1,0:T(8,128)(2,1)}, bf16[512,2048]{1,0:T(8,128)(2,1)}, u32[]{:S(2)}, u32[]{:S(2)}) collective-permute-start(bf16[512,2048]{1,0:T(8,128)(2,1)} %param.9), channel_id=1, source_target_pairs={{0,2},{2,4},{4,6},{6,8},{8,10},{10,12},{12,14},{14,16},{16,18},{18... | collective-permute-start | bytes 6291464 | tf_op jit(solution)/shard_map/ppermute | solution.py:10
  9.2 3.6 %copy-start.4 = (bf16[512,2048]{1,0:T(8,128)(2,1)S(1)}, bf16[512,2048]{1,0:T(8,128)(2,1)}, u32[]{:S(2)}) copy-start(bf16[512,2048]{1,0:T(8,128)(2,1)} %param.10) | copy-start | bytes 6291460
  9.2 53.2 %collective-permute-start.1 = (f32[512,768]{1,0:T(8,128)}, f32[512,768]{1,0:T(8,128)}, u32[]{:S(2)}, u32[]{:S(2)}) collective-permute-start(f32[512,768]{1,0:T(8,128)} %fusion.17), channel_id=1, source_target_pairs={{0,1},{1,0},{2,3},{3,2},{4,5},{5,4},{6,7},{7,6},{8,9},{9,8},{10,11... | collective-permute-start | bytes 4718600 | tf_op jit(solution)/shard_map/ppermute | solution.py:10
  12.2 3.7 %copy-start.13 = (s32[16]{0:T(128)S(1)}, s32[16]{0:T(128)}, u32[]{:S(2)}) copy-start(s32[16]{0:T(128)} %param.14) | copy-start | bytes 196
  12.2 4.9 %copy-start.9 = (s32[16]{0:T(128)S(1)}, s32[16]{0:T(128)}, u32[]{:S(2)}) copy-start(s32[16]{0:T(128)} %param.13) | copy-start | bytes 196
  12.2 5.6 %copy-start.7 = (s32[512,8]{0,1:T(8,128)S(1)}, s32[512,8]{0,1:T(8,128)}, u32[]{:S(2)}) copy-start(s32[512,8]{0,1:T(8,128)} %param.11) | copy-start | bytes 49156
  12.2 5.6 %copy-start.8 = (bf16[512,8]{0,1:T(8,128)(2,1)S(1)}, bf16[512,8]{0,1:T(8,128)(2,1)}, u32[]{:S(2)}) copy-start(bf16[512,8]{0,1:T(8,128)(2,1)} %param.12) | copy-start | bytes 24580
  12.2 50.2 %collective-permute-start = (f32[512,768]{1,0:T(8,128)}, f32[512,768]{1,0:T(8,128)}, u32[]{:S(2)}, u32[]{:S(2)}) collective-permute-start(f32[512,768]{1,0:T(8,128)} %fusion.25), channel_id=1, source_target_pairs={{0,1},{1,0},{2,3},{3,2},{4,5},{5,4},{6,7},{7,6},{8,9},{9,8},{10,11... | collective-permute-start | bytes 4718600 | tf_op jit(solution)/shard_map/ppermute | solution.py:10
  15.8 46.9 %collective-permute-start.2 = (f32[512,768]{1,0:T(8,128)}, f32[512,768]{1,0:T(8,128)}, u32[]{:S(2)}, u32[]{:S(2)}) collective-permute-start(f32[512,768]{1,0:T(8,128)} %fusion.7), channel_id=1, source_target_pairs={{0,1},{1,0},{2,3},{3,2},{4,5},{5,4},{6,7},{7,6},{8,9},{9,8},{10,11... | collective-permute-start | bytes 4718600 | tf_op jit(solution)/shard_map/ppermute | solution.py:10
  19.1 39.0 %copy-start.3 = (bf16[1,768,2048]{2,1,0:T(8,128)(2,1)S(1)}, bf16[1,768,2048]{2,1,0:T(8,128)(2,1)}, u32[]{:S(2)}) copy-start(bf16[1,768,2048]{2,1,0:T(8,128)(2,1)} %param.15) | copy-start | bytes 9437188
  19.1 42.6 %collective-permute-start.3 = (bf16[512]{0:T(512)(128)(2,1)S(1)}, bf16[512]{0:T(512)(128)(2,1)S(1)}, u32[]{:S(2)}, u32[]{:S(2)}) collective-permute-start(bf16[512]{0:T(512)(128)(2,1)S(1)} %multiply_convert_fusion.6), channel_id=1, source_target_pairs={{0,2},{2,4},{4,6},{6,8},{8,10},{10,12},{12,14},{14,16},{16,18},{18... | collective-permute-start | bytes 3080 | tf_op jit(solution)/shard_map/ppermute | solution.py:10
  58.0 4.1 %copy-start.5 = (bf16[512,2048]{1,0:T(8,128)(2,1)S(1)}, bf16[512,2048]{1,0:T(8,128)(2,1)}, u32[]{:S(2)}) copy-start(bf16[512,2048]{1,0:T(8,128)(2,1)} %param.10) | copy-start | bytes 6291460
  58.0 16.6 %collective-permute-start.6 = (f32[512,768]{1,0:T(8,128)S(1)}, f32[512,768]{1,0:T(8,128)S(1)}, u32[]{:S(2)}, u32[]{:S(2)}) collective-permute-start(f32[512,768]{1,0:T(8,128)S(1)} %fusion.13), channel_id=1, source_target_pairs={{0,1},{1,0},{2,3},{3,2},{4,5},{5,4},{6,7},{7,6},{8,9},{9,8},{10,11... | collective-permute-start | bytes 4718600 | tf_op jit(solution)/shard_map/ppermute | solution.py:10
  61.7 13.0 %collective-permute-start.5 = (f32[512,768]{1,0:T(8,128)S(1)}, f32[512,768]{1,0:T(8,128)S(1)}, u32[]{:S(2)}, u32[]{:S(2)}) collective-permute-start(f32[512,768]{1,0:T(8,128)S(1)} %fusion.21), channel_id=1, source_target_pairs={{0,1},{1,0},{2,3},{3,2},{4,5},{5,4},{6,7},{7,6},{8,9},{9,8},{10,11... | collective-permute-start | bytes 4718600 | tf_op jit(solution)/shard_map/ppermute | solution.py:10
  62.4 14.8 %collective-permute-start.9 = (bf16[32,2048]{1,0:T(8,128)(2,1)S(1)}, bf16[32,2048]{1,0:T(8,128)(2,1)S(1)}, u32[]{:S(2)}, u32[]{:S(2)}) collective-permute-start(bf16[32,2048]{1,0:T(8,128)(2,1)S(1)} %slice.16), channel_id=1, source_target_pairs={{0,2},{2,4},{4,6},{6,8},{8,10},{10,12},{12,14},{14,16},{16,18},{18... | collective-permute-start | bytes 393224 | tf_op jit(solution)/shard_map/ppermute | solution.py:10
  62.4 51.3 %collective-permute-start.8 = (bf16[480,2048]{1,0:T(8,128)(2,1)S(1)}, bf16[480,2048]{1,0:T(8,128)(2,1)S(1)}, u32[]{:S(2)}, u32[]{:S(2)}) collective-permute-start(bf16[480,2048]{1,0:T(8,128)(2,1)S(1)} %slice.15), channel_id=1, source_target_pairs={{0,2},{2,4},{4,6},{6,8},{8,10},{10,12},{12,14},{14,16},{16,18},{18... | collective-permute-start | bytes 5898248 | tf_op jit(solution)/shard_map/ppermute | solution.py:10
  62.7 4.9 %copy-start.12 = (bf16[512,2048]{1,0:T(8,128)(2,1)S(1)}, bf16[512,2048]{1,0:T(8,128)(2,1)}, u32[]{:S(2)}) copy-start(bf16[512,2048]{1,0:T(8,128)(2,1)} %param.9) | copy-start | bytes 6291460
  115.7 9.4 %collective-permute-start.10 = (f32[512,768]{1,0:T(8,128)S(1)}, f32[512,768]{1,0:T(8,128)S(1)}, u32[]{:S(2)}, u32[]{:S(2)}) collective-permute-start(f32[512,768]{1,0:T(8,128)S(1)} %fusion.3), channel_id=1, source_target_pairs={{0,1},{1,0},{2,3},{3,2},{4,5},{5,4},{6,7},{7,6},{8,9},{9,8},{10,11... | collective-permute-start | bytes 4718600 | tf_op jit(solution)/shard_map/ppermute | solution.py:10
  119.3 1.9 copy-start.10
  125.0 48.6 %collective-permute-start.7 = (bf16[512,2048]{1,0:T(8,128)(2,1)S(1)}, bf16[512,2048]{1,0:T(8,128)(2,1)S(1)}, u32[]{:S(2)}, u32[]{:S(2)}) collective-permute-start(bf16[512,2048]{1,0:T(8,128)(2,1)S(1)} %fusion.30), channel_id=1, source_target_pairs={{0,30},{2,0},{4,2},{6,4},{8,6},{10,8},{12,10},{14,12},{16,14},{18,... | collective-permute-start | bytes 6291464 | tf_op jit(solution)/shard_map/ppermute | solution.py:10
  129.9 1.9 copy-start.16
  130.1 5.7 %copy-start.15 = (bf16[768,2048]{1,0:T(8,128)(2,1)S(1)}, bf16[768,2048]{1,0:T(8,128)(2,1)}, u32[]{:S(2)}) copy-start(bf16[768,2048]{1,0:T(8,128)(2,1)} %convolution_convert_fusion.5) | copy-start | bytes 9437188
  130.1 82.8 %collective-permute-start.11 = (bf16[448,2048]{1,0:T(8,128)(2,1)S(1)}, bf16[448,2048]{1,0:T(8,128)(2,1)S(1)}, u32[]{:S(2)}, u32[]{:S(2)}) collective-permute-start(bf16[448,2048]{1,0:T(8,128)(2,1)S(1)} %slice.20), channel_id=1, source_target_pairs={{0,30},{2,0},{4,2},{6,4},{8,6},{10,8},{12,10},{14,12},{16,14},{18,... | collective-permute-start | bytes 5505032 | tf_op jit(solution)/shard_map/ppermute | solution.py:10
  135.3 5.9 %copy-start.14 = (bf16[768,2048]{1,0:T(8,128)(2,1)S(1)}, bf16[768,2048]{1,0:T(8,128)(2,1)}, u32[]{:S(2)}) copy-start(bf16[768,2048]{1,0:T(8,128)(2,1)} %convolution_convert_fusion.4) | copy-start | bytes 9437188
  135.3 82.7 %collective-permute-start.12 = (bf16[64,2048]{1,0:T(8,128)(2,1)S(1)}, bf16[64,2048]{1,0:T(8,128)(2,1)S(1)}, u32[]{:S(2)}, u32[]{:S(2)}) collective-permute-start(bf16[64,2048]{1,0:T(8,128)(2,1)S(1)} %slice.21), channel_id=1, source_target_pairs={{0,30},{2,0},{4,2},{6,4},{8,6},{10,8},{12,10},{14,12},{16,14},{18,... | collective-permute-start | bytes 786440 | tf_op jit(solution)/shard_map/ppermute | solution.py:10
  212.9 6.5 %copy-start.1 = (bf16[1,768,2048]{2,1,0:T(8,128)(2,1)S(1)}, bf16[1,768,2048]{2,1,0:T(8,128)(2,1)}, u32[]{:S(2)}) copy-start(bf16[1,768,2048]{2,1,0:T(8,128)(2,1)} %param.17) | copy-start | bytes 9437188
  218.1 1.3 copy-start.6

commit v3 on v2

--- a/solution.py
+++ b/solution.py
@@ -8,6 +8,10 @@
     count = lax.axis_size(axis)
     pairs = [(source, (source + steps) % count) for source in range(count)]
     return lax.ppermute(value, axis, pairs)
+
+
+def edge_pairs(count):
+    return [(source, source + 1) for source in range(count - 1)], [(count - 1, 0)]
 
 
 def route_weight(route_ids, weights_in, expert):
@@ -99,7 +103,11 @@
     next_dy = take_rows(cotangent, next_index)
     dy_cut = capacity - capacity // 16
     cut = capacity - capacity // 8
-    far_dy_head = passed_along(next_dy[:dy_cut], "expert", 1)
+    gate_cut = dy_cut - capacity // 32
+    far_dy_head = passed_along(next_dy[:gate_cut], "expert", 1)
+    near, wrapped = edge_pairs(columns)
+    dy_near = lax.ppermute(next_dy[gate_cut:dy_cut], "expert", near)
+    dy_wrapped = lax.ppermute(next_dy[gate_cut:dy_cut], "expert", wrapped)
     far_dy_tail = passed_along(next_dy[dy_cut:], "expert", 1)
     own_w, far_w = own_weight[:, None], far_w.astype(jnp.float32)[:, None]
 
@@ -121,8 +129,11 @@
     far_out = hidden_by_weights(far_act, wd).astype(jnp.bfloat16)
     next_out = passed_along(far_out, "expert", -1)
 
-    far_dy_head, far_dy_tail, far_out = lax.optimization_barrier((far_dy_head, far_dy_tail, far_out))
-    far_dy = jnp.concatenate([far_dy_head, far_dy_tail])
+    far_dy_head, dy_near, dy_wrapped, far_dy_tail, far_out = lax.optimization_barrier(
+        (far_dy_head, dy_near, dy_wrapped, far_dy_tail, far_out)
+    )
+    dy_gate = jnp.where(column == 0, dy_wrapped, dy_near)
+    far_dy = jnp.concatenate([far_dy_head, dy_gate, far_dy_tail])
     far_back = rows_by_weights(far_dy, wd)
     far_back = summed_over_dp(far_back)
     far_dgate, far_dup = slopes_of(far_gate, far_up, far_back, far_w)

time: 220 us -> 228 us (1.036)
  starting transfers between devices: 7.24 us -> 17 us
  waiting for transfers between devices: 138 us -> 131 us
  other arithmetic: 11.6 us -> 16 us
    ppermute x13, waiting for transfers between devices: 138 us -> 131 us  [passed_along(): return lax.ppermute(value, axis, pairs)]
    ppermute x13, starting transfers between devices: 7.24 us -> 14.4 us  [passed_along(): return lax.ppermute(value, axis, pairs)]
    convert_element_type x1, other arithmetic: 0.72 us -> 3.37 us  [act_of(): (weight_col * (gate_val * jax.nn.sigmoid(gate_val)) * up_val).astype(jnp....]
    ppermute x0 -> x2, starting transfers between devices: none -> 2.59 us  [the longest x1 1.29 us: per_device(): dy_near = lax.ppermute(next_dy[gate_cut:dy_cut], 'expert', near)]
  transfers between devices with their start and end apart: 13 -> 15, of which waited for: 5 -> 5; matrix products, arithmetic and copies ran while one was open for 31% -> 33% of each run, Pallas kernels for 0% -> 0%
where the time goes in v3:
time: 228 us
  waiting for transfers between devices  131 us (57%)
  matrix products  56.4 us (25%)
  starting transfers between devices  17 us (7%)
  other arithmetic  16 us (7%)
  local copies, waits for them, and re-layouts  5.83 us (3%)
    ppermute x13, waiting for transfers between devices, passed_along(): return lax.ppermute(value, axis, pairs)  131 us
    dot_general x6, matrix products, over_rows(): lax.dot_general(hidden, rows, (((0,), (0,)), ((), ())), preferred_element...  22.8 us
    dot_general x6, matrix products, rows_by_weights(): lax.dot_general(rows, weight, (((1,), (1,)), ((), ())), preferred_element...  22.5 us
    ppermute x13, starting transfers between devices, passed_along(): return lax.ppermute(value, axis, pairs)  14.4 us
    dot_general x6, matrix products, hidden_by_weights(): return jnp.dot(hidden, weight, preferred_element_type=jnp.float32)  11 us
    convert_element_type x2, other arithmetic, slopes_of(): return (grad_gate.astype(jnp.bfloat16), grad_up.astype(jnp.bfloat16))  7.86 us
  transfers between devices with their start and end apart: 15, of which 5 were waited for; matrix products, arithmetic and copies ran while one was open for 33% of the time, Pallas kernels for 0%

profile of v3, /device:TPU:0, one launch (start us, length us, event | category | flops | bytes accessed | tf_op | source)
XLA Modules:
  0.0 227.8 jit_solution(654446801198933140)
XLA Ops:
  0.7 3.0 %collective-permute-start.4 = (bf16[512,2048]{1,0:T(8,128)(2,1)}, bf16[512,2048]{1,0:T(8,128)(2,1)}, u32[]{:S(2)}, u32[]{:S(2)}) collective-permute-start(bf16[512,2048]{1,0:T(8,128)(2,1)} %param.9), channel_id=1, source_target_pairs={{0,2},{2,4},{4,6},{6,8},{8,10},{10,12},{12,14},{14,16},{16,18},{18... | collective-permute-start | bytes 6291464 | tf_op jit(solution)/shard_map/ppermute | solution.py:10
  3.7 4.6 %fusion.7 = f32[512,768]{1,0:T(8,128)} fusion(bf16[512,2048]{1,0:T(8,128)(2,1)} %param.10, bf16[1,768,2048]{2,1,0:T(8,128)(2,1)S(1)} %copy-done), kind=kOutput, calls=%fused_computation.19 | convolution fusion | flops 1610612736 | bytes 6815744 | tf_op jit(solution)/shard_map/dot_general | solution.py:54
  8.3 3.0 %fusion.17 = f32[512,768]{1,0:T(8,128)} fusion(bf16[512,2048]{1,0:T(8,128)(2,1)S(1)} %copy-done.12, bf16[1,768,2048]{2,1,0:T(8,128)(2,1)S(1)} %copy-done.10), kind=kOutput, calls=%fused_computation.29 | convolution fusion | flops 1610612736 | bytes 6815744 | tf_op jit(solution)/shard_map/dot_general | solution.py:54
  11.3 0.6 collective-permute-start.1
  11.8 3.0 %fusion.25 = f32[512,768]{1,0:T(8,128)} fusion(bf16[512,2048]{1,0:T(8,128)(2,1)S(1)} %copy-done.12, bf16[1,768,2048]{2,1,0:T(8,128)(2,1)S(1)} %copy-done.2), kind=kOutput, calls=%fused_computation.37 | convolution fusion | flops 1610612736 | bytes 6815744 | tf_op jit(solution)/shard_map/dot_general | solution.py:54
  14.8 0.6 dynamic_slice.3
  16.1 0.6 fusion.41
  16.7 1.3 fusion.39
  18.1 2.4 %collective-permute-start.3 = (bf16[512]{0:T(512)(128)(2,1)S(1)}, bf16[512]{0:T(512)(128)(2,1)S(1)}, u32[]{:S(2)}, u32[]{:S(2)}) collective-permute-start(bf16[512]{0:T(512)(128)(2,1)S(1)} %multiply_convert_fusion.6), channel_id=1, source_target_pairs={{0,2},{2,4},{4,6},{6,8},{8,10},{10,12},{12,14},{14,16},{16,18},{18... | collective-permute-start | bytes 3080 | tf_op jit(solution)/shard_map/ppermute | solution.py:10
  20.5 33.1 %collective-permute-done.4 = bf16[512,2048]{1,0:T(8,128)(2,1)} collective-permute-done((bf16[512,2048]{1,0:T(8,128)(2,1)}, bf16[512,2048]{1,0:T(8,128)(2,1)}, u32[]{:S(2)}, u32[]{:S(2)}) %collective-permute-start.4) | collective-permute-done | bytes 2097184 | tf_op jit(solution)/shard_map/ppermute | solution.py:10
  53.6 5.5 %fusion.13 = f32[512,768]{1,0:T(8,128)} fusion(bf16[512,2048]{1,0:T(8,128)(2,1)} %collective-permute-done.4, bf16[1,768,2048]{2,1,0:T(8,128)(2,1)} %param.16), kind=kOutput, calls=%fused_computation.25 | convolution fusion | flops 1610612736 | bytes 6815744 | tf_op jit(solution)/shard_map/dot_general | solution.py:54
  59.2 4.6 %fusion.21 = f32[512,768]{1,0:T(8,128)} fusion(bf16[512,2048]{1,0:T(8,128)(2,1)} %collective-permute-done.4, bf16[1,768,2048]{2,1,0:T(8,128)(2,1)S(1)} %copy-done.3), kind=kOutput, calls=%fused_computation.33 | convolution fusion | flops 1610612736 | bytes 6815744 | tf_op jit(solution)/shard_map/dot_general | solution.py:54
  63.8 0.5 collective-permute-start.5
  64.3 0.8 slice.20
  65.1 0.9 slice.21
  66.0 1.6 slice.19
  67.7 1.3 collective-permute-start.10
  69.0 1.3 collective-permute-start.9
  70.3 0.4 collective-permute-start.8
  70.7 4.9 %multiply_convert_fusion.4 = (bf16[512,768]{1,0:T(8,128)(2,1)S(1)}, bf16[512,768]{1,0:T(8,128)(2,1)S(1)}, bf16[512,768]{1,0:T(8,128)(2,1)S(1)}) fusion(f32[512,768]{1,0:T(8,128)} %fusion.17, f32[512,768]{1,0:T(8,128)} %collective-permute-done.1, f32[512,768]{1,0:T(8,128)} %fusion.25, f32[512,768]{1,0:T(8,128)} %collective-permute-done, ...), kind=kLoop, calls=%fused_computation.49 | loop fusion | flops 7864320 | bytes 11798528 | tf_op jit(solution)/shard_map/convert_element_type | solution.py:75
  75.6 3.5 %convolution_convert_fusion.5 = bf16[768,2048]{1,0:T(8,128)(2,1)} fusion(bf16[512,768]{1,0:T(8,128)(2,1)S(1)} %get-tuple-element.31, bf16[512,2048]{1,0:T(8,128)(2,1)S(1)} %copy-done.13), kind=kOutput, calls=%fused_computation.11 | convolution fusion | flops 1612185600 | bytes 6029312 | tf_op jit(solution)/shard_map/dot_general | solution.py:62
  79.1 1.8 convolution_convert_fusion.4
  81.0 0.6 collective-permute-start.11
  81.6 3.4 %multiply_convert_fusion.2 = (bf16[512,768]{1,0:T(8,128)(2,1)S(1)}, f32[512,768]{1,0:T(8,128)S(1)}) fusion(f32[512]{0:T(512)S(1)} %convert_element_type.112, f32[512,768]{1,0:T(8,128)} %fusion.21, f32[512,768]{1,0:T(8,128)} %collective-permute-done.5, f32[512,768]{1,0:T(8,128)} %fusion.13, f32[512,768]{1,0:T(8,128)} %collective-permute-done.6), kind=kLoop, calls=%fused_computation.45 | loop fusion | flops 3538944 | bytes 8652800 | tf_op jit(solution)/shard_map/convert_element_type | solution.py:67
  85.0 1.8 fusion.30
  86.9 34.2 %collective-permute-done.11 = bf16[32,2048]{1,0:T(8,128)(2,1)S(1)} collective-permute-done((bf16[32,2048]{1,0:T(8,128)(2,1)S(1)}, bf16[32,2048]{1,0:T(8,128)(2,1)S(1)}, u32[]{:S(2)}, u32[]{:S(2)}) %collective-permute-start.11) | collective-permute-done | bytes 131104 | tf_op jit(solution)/shard_map/ppermute | solution.py:10
  121.0 1.9 fusion.3
  123.0 3.5 %convolution_convert_fusion.3 = bf16[768,2048]{1,0:T(8,128)(2,1)} fusion(bf16[512,768]{1,0:T(8,128)(2,1)S(1)} %get-tuple-element.33, bf16[512,2048]{1,0:T(8,128)(2,1)S(1)} %copy-done.5), kind=kOutput, calls=%fused_computation.9 | convolution fusion | flops 1612185600 | bytes 6029312 | tf_op jit(solution)/shard_map/dot_general | solution.py:62
  126.6 1.8 fusion.9
  128.4 1.8 fusion.15
  130.3 1.9 fusion.27
  132.2 3.7 %collective-permute-start.7 = (bf16[512,2048]{1,0:T(8,128)(2,1)S(1)}, bf16[512,2048]{1,0:T(8,128)(2,1)S(1)}, u32[]{:S(2)}, u32[]{:S(2)}) collective-permute-start(bf16[512,2048]{1,0:T(8,128)(2,1)S(1)} %fusion.30), channel_id=1, source_target_pairs={{0,30},{2,0},{4,2},{6,4},{8,6},{10,8},{12,10},{14,12},{16,14},{18,... | collective-permute-start | bytes 6291464 | tf_op jit(solution)/shard_map/ppermute | solution.py:10
  135.9 2.9 %multiply_convert_fusion.1 = (bf16[512,768]{1,0:T(8,128)(2,1)S(1)}, bf16[512,768]{1,0:T(8,128)(2,1)S(1)}) fusion(f32[512,768]{1,0:T(8,128)S(1)} %get-tuple-element.28, f32[512,768]{1,0:T(8,128)} %fusion.21, f32[512,768]{1,0:T(8,128)} %collective-permute-done.5, f32[512]{0:T(512)S(1)} %convert_element_type.112, f32[512,768]{1,0:T(8,128)S(1)} %fusion.3, ...), kind=kLoop, calls=%fused_computation.43 | loop fusion | flops 6291456 | bytes 9439232 | tf_op jit(solution)/shard_map/convert_element_type | solution.py:75
  138.8 1.8 fusion.11
  140.6 1.9 add_convert_fusion.4
  142.5 0.1 slice.25
  142.7 1.6 collective-permute-start.13
  144.2 0.2 copy-done.16
  144.4 3.6 %fusion.2 = bf16[1,768,2048]{2,1,0:T(8,128)(2,1)} fusion(bf16[768,2048]{1,0:T(8,128)(2,1)S(1)} %copy-done.16, bf16[512,768]{1,0:T(8,128)(2,1)S(1)} %get-tuple-element.27, bf16[32,2048]{1,0:T(8,128)(2,1)S(1)} %collective-permute-done.11, bf16[16,2048]{1,0:T(8,128)(2,1)S(1)} %broadcast_select_fusion, bf16[464,2048]{1,0:T(8,128)(2,1)S(1)} %collective-permute-done.8), kind=kOutput, calls=%fused_computation.14 | convolution fusion | flops 1624768512 | bytes 9175040 | tf_op jit(solution)/shard_map/dot_general | solution.py:62
  148.1 1.6 collective-permute-start.14
  149.6 5.2 %fusion = bf16[1,768,2048]{2,1,0:T(8,128)(2,1)} fusion(bf16[768,2048]{1,0:T(8,128)(2,1)S(1)} %copy-done.15, bf16[512,768]{1,0:T(8,128)(2,1)S(1)} %get-tuple-element.29, bf16[512,2048]{1,0:T(8,128)(2,1)} %collective-permute-done.4), kind=kOutput, calls=%fused_computation.12 | convolution fusion | flops 1618477056 | bytes 9175040 | tf_op jit(solution)/shard_map/dot_general | solution.py:62
  154.8 5.2 %fusion.1 = bf16[1,768,2048]{2,1,0:T(8,128)(2,1)} fusion(bf16[768,2048]{1,0:T(8,128)(2,1)S(1)} %convolution_convert_fusion.4, bf16[512,768]{1,0:T(8,128)(2,1)S(1)} %get-tuple-element.30, bf16[512,2048]{1,0:T(8,128)(2,1)} %collective-permute-done.4), kind=kOutput, calls=%fused_computation.13 | convolution fusion | flops 1618477056 | bytes 9175040 | tf_op jit(solution)/shard_map/dot_general | solution.py:62
  160.0 21.9 %collective-permute-done.7 = bf16[512,2048]{1,0:T(8,128)(2,1)S(1)} collective-permute-done((bf16[512,2048]{1,0:T(8,128)(2,1)S(1)}, bf16[512,2048]{1,0:T(8,128)(2,1)S(1)}, u32[]{:S(2)}, u32[]{:S(2)}) %collective-permute-start.7) | collective-permute-done | bytes 2097184 | tf_op jit(solution)/shard_map/ppermute | solution.py:10
  181.9 2.0 add_convert_fusion.5
  183.9 37.3 %collective-permute-done.13 = bf16[448,2048]{1,0:T(8,128)(2,1)S(1)} collective-permute-done((bf16[448,2048]{1,0:T(8,128)(2,1)S(1)}, bf16[448,2048]{1,0:T(8,128)(2,1)S(1)}, u32[]{:S(2)}, u32[]{:S(2)}) %collective-permute-start.13) | collective-permute-done | bytes 1835040 | tf_op jit(solution)/shard_map/ppermute | solution.py:10
  221.2 0.7 add_convert_fusion.3
  221.9 4.5 %collective-permute-done.14 = bf16[64,2048]{1,0:T(8,128)(2,1)S(1)} collective-permute-done((bf16[64,2048]{1,0:T(8,128)(2,1)S(1)}, bf16[64,2048]{1,0:T(8,128)(2,1)S(1)}, u32[]{:S(2)}, u32[]{:S(2)}) %collective-permute-start.14) | collective-permute-done | bytes 262176 | tf_op jit(solution)/shard_map/ppermute | solution.py:10
  226.4 1.3 copy-done.6
  (51 shorter events, 0.5 us)
Async XLA Ops:
  0.6 3.1 %copy-start = (bf16[1,768,2048]{2,1,0:T(8,128)(2,1)S(1)}, bf16[1,768,2048]{2,1,0:T(8,128)(2,1)}, u32[]{:S(2)}) copy-start(bf16[1,768,2048]{2,1,0:T(8,128)(2,1)} %param.17) | copy-start | bytes 9437188
  0.6 7.6 %copy-start.12 = (bf16[512,2048]{1,0:T(8,128)(2,1)S(1)}, bf16[512,2048]{1,0:T(8,128)(2,1)}, u32[]{:S(2)}) copy-start(bf16[512,2048]{1,0:T(8,128)(2,1)} %param.9) | copy-start | bytes 6291460
  0.7 7.6 %copy-start.10 = (bf16[1,768,2048]{2,1,0:T(8,128)(2,1)S(1)}, bf16[1,768,2048]{2,1,0:T(8,128)(2,1)}, u32[]{:S(2)}) copy-start(bf16[1,768,2048]{2,1,0:T(8,128)(2,1)} %param.16) | copy-start | bytes 9437188
  0.7 53.0 %collective-permute-start.4 = (bf16[512,2048]{1,0:T(8,128)(2,1)}, bf16[512,2048]{1,0:T(8,128)(2,1)}, u32[]{:S(2)}, u32[]{:S(2)}) collective-permute-start(bf16[512,2048]{1,0:T(8,128)(2,1)} %param.9), channel_id=1, source_target_pairs={{0,2},{2,4},{4,6},{6,8},{8,10},{10,12},{12,14},{14,16},{16,18},{18... | collective-permute-start | bytes 6291464 | tf_op jit(solution)/shard_map/ppermute | solution.py:10
  8.3 3.6 %copy-start.2 = (bf16[1,768,2048]{2,1,0:T(8,128)(2,1)S(1)}, bf16[1,768,2048]{2,1,0:T(8,128)(2,1)}, u32[]{:S(2)}) copy-start(bf16[1,768,2048]{2,1,0:T(8,128)(2,1)} %param.15) | copy-start | bytes 9437188
  8.3 59.4 %collective-permute-start.2 = (f32[512,768]{1,0:T(8,128)}, f32[512,768]{1,0:T(8,128)}, u32[]{:S(2)}, u32[]{:S(2)}) collective-permute-start(f32[512,768]{1,0:T(8,128)} %fusion.7), channel_id=1, source_target_pairs={{0,1},{1,0},{2,3},{3,2},{4,5},{5,4},{6,7},{7,6},{8,9},{9,8},{10,11... | collective-permute-start | bytes 4718600 | tf_op jit(solution)/shard_map/ppermute | solution.py:10
  11.3 3.6 %copy-start.14 = (s32[16]{0:T(128)S(1)}, s32[16]{0:T(128)}, u32[]{:S(2)}) copy-start(s32[16]{0:T(128)} %param.14) | copy-start | bytes 196
  11.3 4.8 %copy-start.9 = (s32[16]{0:T(128)S(1)}, s32[16]{0:T(128)}, u32[]{:S(2)}) copy-start(s32[16]{0:T(128)} %param.13) | copy-start | bytes 196
  11.3 5.5 %copy-start.7 = (s32[512,8]{0,1:T(8,128)S(1)}, s32[512,8]{0,1:T(8,128)}, u32[]{:S(2)}) copy-start(s32[512,8]{0,1:T(8,128)} %param.11) | copy-start | bytes 49156
  11.3 5.5 %copy-start.8 = (bf16[512,8]{0,1:T(8,128)(2,1)S(1)}, bf16[512,8]{0,1:T(8,128)(2,1)}, u32[]{:S(2)}) copy-start(bf16[512,8]{0,1:T(8,128)(2,1)} %param.12) | copy-start | bytes 24580
  11.3 57.7 %collective-permute-start.1 = (f32[512,768]{1,0:T(8,128)}, f32[512,768]{1,0:T(8,128)}, u32[]{:S(2)}, u32[]{:S(2)}) collective-permute-start(f32[512,768]{1,0:T(8,128)} %fusion.17), channel_id=1, source_target_pairs={{0,1},{1,0},{2,3},{3,2},{4,5},{5,4},{6,7},{7,6},{8,9},{9,8},{10,11... | collective-permute-start | bytes 4718600 | tf_op jit(solution)/shard_map/ppermute | solution.py:10
  14.8 55.5 %collective-permute-start = (f32[512,768]{1,0:T(8,128)}, f32[512,768]{1,0:T(8,128)}, u32[]{:S(2)}, u32[]{:S(2)}) collective-permute-start(f32[512,768]{1,0:T(8,128)} %fusion.25), channel_id=1, source_target_pairs={{0,1},{1,0},{2,3},{3,2},{4,5},{5,4},{6,7},{7,6},{8,9},{9,8},{10,11... | collective-permute-start | bytes 4718600 | tf_op jit(solution)/shard_map/ppermute | solution.py:10
  18.1 41.1 %copy-start.3 = (bf16[1,768,2048]{2,1,0:T(8,128)(2,1)S(1)}, bf16[1,768,2048]{2,1,0:T(8,128)(2,1)}, u32[]{:S(2)}) copy-start(bf16[1,768,2048]{2,1,0:T(8,128)(2,1)} %param.15) | copy-start | bytes 9437188
  18.1 45.7 %collective-permute-start.3 = (bf16[512]{0:T(512)(128)(2,1)S(1)}, bf16[512]{0:T(512)(128)(2,1)S(1)}, u32[]{:S(2)}, u32[]{:S(2)}) collective-permute-start(bf16[512]{0:T(512)(128)(2,1)S(1)} %multiply_convert_fusion.6), channel_id=1, source_target_pairs={{0,2},{2,4},{4,6},{6,8},{8,10},{10,12},{12,14},{14,16},{16,18},{18... | collective-permute-start | bytes 3080 | tf_op jit(solution)/shard_map/ppermute | solution.py:10
  59.2 21.8 %collective-permute-start.6 = (f32[512,768]{1,0:T(8,128)}, f32[512,768]{1,0:T(8,128)}, u32[]{:S(2)}, u32[]{:S(2)}) collective-permute-start(f32[512,768]{1,0:T(8,128)} %fusion.13), channel_id=1, source_target_pairs={{0,1},{1,0},{2,3},{3,2},{4,5},{5,4},{6,7},{7,6},{8,9},{9,8},{10,11... | collective-permute-start | bytes 4718600 | tf_op jit(solution)/shard_map/ppermute | solution.py:10
  63.8 17.9 %collective-permute-start.5 = (f32[512,768]{1,0:T(8,128)}, f32[512,768]{1,0:T(8,128)}, u32[]{:S(2)}, u32[]{:S(2)}) collective-permute-start(f32[512,768]{1,0:T(8,128)} %fusion.21), channel_id=1, source_target_pairs={{0,1},{1,0},{2,3},{3,2},{4,5},{5,4},{6,7},{7,6},{8,9},{9,8},{10,11... | collective-permute-start | bytes 4718600 | tf_op jit(solution)/shard_map/ppermute | solution.py:10
  67.7 19.1 %collective-permute-start.10 = (bf16[16,2048]{1,0:T(8,128)(2,1)S(1)}, bf16[16,2048]{1,0:T(8,128)(2,1)S(1)}, u32[]{:S(2)}, u32[]{:S(2)}) collective-permute-start(bf16[16,2048]{1,0:T(8,128)(2,1)S(1)} %slice.20), channel_id=1, source_target_pairs={{30,0},{31,1}} | collective-permute-start | bytes 196616 | tf_op jit(solution)/shard_map/ppermute | solution.py:110
  69.0 17.8 %collective-permute-start.9 = (bf16[16,2048]{1,0:T(8,128)(2,1)S(1)}, bf16[16,2048]{1,0:T(8,128)(2,1)S(1)}, u32[]{:S(2)}, u32[]{:S(2)}) collective-permute-start(bf16[16,2048]{1,0:T(8,128)(2,1)S(1)} %slice.20), channel_id=1, source_target_pairs={{0,2},{2,4},{4,6},{6,8},{8,10},{10,12},{12,14},{14,16},{16,18},{18... | collective-permute-start | bytes 196616 | tf_op jit(solution)/shard_map/ppermute | solution.py:109
  70.3 50.7 %collective-permute-start.8 = (bf16[464,2048]{1,0:T(8,128)(2,1)S(1)}, bf16[464,2048]{1,0:T(8,128)(2,1)S(1)}, u32[]{:S(2)}, u32[]{:S(2)}) collective-permute-start(bf16[464,2048]{1,0:T(8,128)(2,1)S(1)} %slice.19), channel_id=1, source_target_pairs={{0,2},{2,4},{4,6},{6,8},{8,10},{10,12},{12,14},{14,16},{16,18},{18... | collective-permute-start | bytes 5701640 | tf_op jit(solution)/shard_map/ppermute | solution.py:10
  70.7 4.9 %copy-start.13 = (bf16[512,2048]{1,0:T(8,128)(2,1)S(1)}, bf16[512,2048]{1,0:T(8,128)(2,1)}, u32[]{:S(2)}) copy-start(bf16[512,2048]{1,0:T(8,128)(2,1)} %param.9) | copy-start | bytes 6291460
  81.0 40.0 %collective-permute-start.11 = (bf16[32,2048]{1,0:T(8,128)(2,1)S(1)}, bf16[32,2048]{1,0:T(8,128)(2,1)S(1)}, u32[]{:S(2)}, u32[]{:S(2)}) collective-permute-start(bf16[32,2048]{1,0:T(8,128)(2,1)S(1)} %slice.21), channel_id=1, source_target_pairs={{0,2},{2,4},{4,6},{6,8},{8,10},{10,12},{12,14},{14,16},{16,18},{18... | collective-permute-start | bytes 393224 | tf_op jit(solution)/shard_map/ppermute | solution.py:10
  121.0 2.0 copy-start.5
  122.9 12.9 %collective-permute-start.12 = (f32[512,768]{1,0:T(8,128)S(1)}, f32[512,768]{1,0:T(8,128)S(1)}, u32[]{:S(2)}, u32[]{:S(2)}) collective-permute-start(f32[512,768]{1,0:T(8,128)S(1)} %fusion.3), channel_id=1, source_target_pairs={{0,1},{1,0},{2,3},{3,2},{4,5},{5,4},{6,7},{7,6},{8,9},{9,8},{10,11... | collective-permute-start | bytes 4718600 | tf_op jit(solution)/shard_map/ppermute | solution.py:10
  126.6 1.9 copy-start.11
  128.4 1.9 copy-start.4
  132.2 49.7 %collective-permute-start.7 = (bf16[512,2048]{1,0:T(8,128)(2,1)S(1)}, bf16[512,2048]{1,0:T(8,128)(2,1)S(1)}, u32[]{:S(2)}, u32[]{:S(2)}) collective-permute-start(bf16[512,2048]{1,0:T(8,128)(2,1)S(1)} %fusion.30), channel_id=1, source_target_pairs={{0,30},{2,0},{4,2},{6,4},{8,6},{10,8},{12,10},{14,12},{16,14},{18,... | collective-permute-start | bytes 6291464 | tf_op jit(solution)/shard_map/ppermute | solution.py:10
  142.5 1.9 copy-start.16
  142.7 7.0 %copy-start.15 = (bf16[768,2048]{1,0:T(8,128)(2,1)S(1)}, bf16[768,2048]{1,0:T(8,128)(2,1)}, u32[]{:S(2)}) copy-start(bf16[768,2048]{1,0:T(8,128)(2,1)} %convolution_convert_fusion.5) | copy-start | bytes 9437188
  142.7 78.5 %collective-permute-start.13 = (bf16[448,2048]{1,0:T(8,128)(2,1)S(1)}, bf16[448,2048]{1,0:T(8,128)(2,1)S(1)}, u32[]{:S(2)}, u32[]{:S(2)}) collective-permute-start(bf16[448,2048]{1,0:T(8,128)(2,1)S(1)} %slice.25), channel_id=1, source_target_pairs={{0,30},{2,0},{4,2},{6,4},{8,6},{10,8},{12,10},{14,12},{16,14},{18,... | collective-permute-start | bytes 5505032 | tf_op jit(solution)/shard_map/ppermute | solution.py:10
  148.1 78.3 %collective-permute-start.14 = (bf16[64,2048]{1,0:T(8,128)(2,1)S(1)}, bf16[64,2048]{1,0:T(8,128)(2,1)S(1)}, u32[]{:S(2)}, u32[]{:S(2)}) collective-permute-start(bf16[64,2048]{1,0:T(8,128)(2,1)S(1)} %slice.26), channel_id=1, source_target_pairs={{0,30},{2,0},{4,2},{6,4},{8,6},{10,8},{12,10},{14,12},{16,14},{18,... | collective-permute-start | bytes 786440 | tf_op jit(solution)/shard_map/ppermute | solution.py:10
  221.2 6.5 %copy-start.1 = (bf16[1,768,2048]{2,1,0:T(8,128)(2,1)S(1)}, bf16[1,768,2048]{2,1,0:T(8,128)(2,1)}, u32[]{:S(2)}) copy-start(bf16[1,768,2048]{2,1,0:T(8,128)(2,1)} %param.17) | copy-start | bytes 9437188
  226.4 1.3 copy-start.6

commit v4 on v3

--- a/solution.py
+++ b/solution.py
@@ -101,9 +101,9 @@
     far_x = passed_along(take_rows(tokens, next_index), "expert", 1)
     far_w = passed_along(next_weight.astype(jnp.bfloat16), "expert", 1)
     next_dy = take_rows(cotangent, next_index)
-    dy_cut = capacity - capacity // 16
-    cut = capacity - capacity // 8
-    gate_cut = dy_cut - capacity // 32
+    dy_cut = capacity - 5 * capacity // 64
+    cut = capacity - 8 * capacity // 64
+    gate_cut = dy_cut - 2 * capacity // 64
     far_dy_head = passed_along(next_dy[:gate_cut], "expert", 1)
     near, wrapped = edge_pairs(columns)
     dy_near = lax.ppermute(next_dy[gate_cut:dy_cut], "expert", near)

time: 228 us -> 228 us (level)
  no operation moved by 1% of the time
where the time goes in v4:
time: 228 us
  waiting for transfers between devices  131 us (57%)
  matrix products  56.4 us (25%)
  starting transfers between devices  17 us (7%)
  other arithmetic  16 us (7%)
  local copies, waits for them, and re-layouts  5.83 us (3%)
    ppermute x13, waiting for transfers between devices, passed_along(): return lax.ppermute(value, axis, pairs)  131 us
    dot_general x6, matrix products, over_rows(): lax.dot_general(hidden, rows, (((0,), (0,)), ((), ())), preferred_element...  22.8 us
    dot_general x6, matrix products, rows_by_weights(): lax.dot_general(rows, weight, (((1,), (1,)), ((), ())), preferred_element...  22.5 us
    ppermute x13, starting transfers between devices, passed_along(): return lax.ppermute(value, axis, pairs)  14.4 us
    dot_general x6, matrix products, hidden_by_weights(): return jnp.dot(hidden, weight, preferred_element_type=jnp.float32)  11 us
    convert_element_type x2, other arithmetic, slopes_of(): return (grad_gate.astype(jnp.bfloat16), grad_up.astype(jnp.bfloat16))  7.86 us
  transfers between devices with their start and end apart: 15, of which 5 were waited for; matrix products, arithmetic and copies ran while one was open for 33% of the time, Pallas kernels for 0%

profile of v4, /device:TPU:0, one launch (start us, length us, event | category | flops | bytes accessed | tf_op | source)
XLA Modules:
  0.0 227.8 jit_solution(2363026591068729298)
XLA Ops:
  0.7 3.0 %collective-permute-start.4 = (bf16[512,2048]{1,0:T(8,128)(2,1)}, bf16[512,2048]{1,0:T(8,128)(2,1)}, u32[]{:S(2)}, u32[]{:S(2)}) collective-permute-start(bf16[512,2048]{1,0:T(8,128)(2,1)} %param.9), channel_id=1, source_target_pairs={{0,2},{2,4},{4,6},{6,8},{8,10},{10,12},{12,14},{14,16},{16,18},{18... | collective-permute-start | bytes 6291464 | tf_op jit(solution)/shard_map/ppermute | solution.py:10
  3.7 4.6 %fusion.7 = f32[512,768]{1,0:T(8,128)} fusion(bf16[512,2048]{1,0:T(8,128)(2,1)} %param.10, bf16[1,768,2048]{2,1,0:T(8,128)(2,1)S(1)} %copy-done), kind=kOutput, calls=%fused_computation.19 | convolution fusion | flops 1610612736 | bytes 6815744 | tf_op jit(solution)/shard_map/dot_general | solution.py:54
  8.3 3.0 %fusion.17 = f32[512,768]{1,0:T(8,128)} fusion(bf16[512,2048]{1,0:T(8,128)(2,1)S(1)} %copy-done.12, bf16[1,768,2048]{2,1,0:T(8,128)(2,1)S(1)} %copy-done.10), kind=kOutput, calls=%fused_computation.29 | convolution fusion | flops 1610612736 | bytes 6815744 | tf_op jit(solution)/shard_map/dot_general | solution.py:54
  11.3 0.6 collective-permute-start.1
  11.8 3.0 %fusion.25 = f32[512,768]{1,0:T(8,128)} fusion(bf16[512,2048]{1,0:T(8,128)(2,1)S(1)} %copy-done.12, bf16[1,768,2048]{2,1,0:T(8,128)(2,1)S(1)} %copy-done.2), kind=kOutput, calls=%fused_computation.37 | convolution fusion | flops 1610612736 | bytes 6815744 | tf_op jit(solution)/shard_map/dot_general | solution.py:54
  14.8 0.6 dynamic_slice.3
  16.1 0.6 fusion.41
  16.7 1.3 fusion.39
  18.1 2.4 %collective-permute-start.3 = (bf16[512]{0:T(512)(128)(2,1)S(1)}, bf16[512]{0:T(512)(128)(2,1)S(1)}, u32[]{:S(2)}, u32[]{:S(2)}) collective-permute-start(bf16[512]{0:T(512)(128)(2,1)S(1)} %multiply_convert_fusion.6), channel_id=1, source_target_pairs={{0,2},{2,4},{4,6},{6,8},{8,10},{10,12},{12,14},{14,16},{16,18},{18... | collective-permute-start | bytes 3080 | tf_op jit(solution)/shard_map/ppermute | solution.py:10
  20.5 33.1 %collective-permute-done.4 = bf16[512,2048]{1,0:T(8,128)(2,1)} collective-permute-done((bf16[512,2048]{1,0:T(8,128)(2,1)}, bf16[512,2048]{1,0:T(8,128)(2,1)}, u32[]{:S(2)}, u32[]{:S(2)}) %collective-permute-start.4) | collective-permute-done | bytes 2097184 | tf_op jit(solution)/shard_map/ppermute | solution.py:10
  53.6 5.5 %fusion.13 = f32[512,768]{1,0:T(8,128)} fusion(bf16[512,2048]{1,0:T(8,128)(2,1)} %collective-permute-done.4, bf16[1,768,2048]{2,1,0:T(8,128)(2,1)} %param.16), kind=kOutput, calls=%fused_computation.25 | convolution fusion | flops 1610612736 | bytes 6815744 | tf_op jit(solution)/shard_map/dot_general | solution.py:54
  59.2 4.6 %fusion.21 = f32[512,768]{1,0:T(8,128)} fusion(bf16[512,2048]{1,0:T(8,128)(2,1)} %collective-permute-done.4, bf16[1,768,2048]{2,1,0:T(8,128)(2,1)S(1)} %copy-done.3), kind=kOutput, calls=%fused_computation.33 | convolution fusion | flops 1610612736 | bytes 6815744 | tf_op jit(solution)/shard_map/dot_general | solution.py:54
  63.8 0.5 collective-permute-start.5
  64.3 0.8 slice.20
  65.1 0.9 slice.21
  66.1 1.6 slice.19
  67.7 1.3 collective-permute-start.10
  69.0 1.3 collective-permute-start.9
  70.3 0.4 collective-permute-start.8
  70.7 4.9 %multiply_convert_fusion.4 = (bf16[512,768]{1,0:T(8,128)(2,1)S(1)}, bf16[512,768]{1,0:T(8,128)(2,1)S(1)}, bf16[512,768]{1,0:T(8,128)(2,1)S(1)}) fusion(f32[512,768]{1,0:T(8,128)} %fusion.17, f32[512,768]{1,0:T(8,128)} %collective-permute-done.1, f32[512,768]{1,0:T(8,128)} %fusion.25, f32[512,768]{1,0:T(8,128)} %collective-permute-done, ...), kind=kLoop, calls=%fused_computation.49 | loop fusion | flops 7864320 | bytes 11798528 | tf_op jit(solution)/shard_map/convert_element_type | solution.py:75
  75.6 3.5 %convolution_convert_fusion.5 = bf16[768,2048]{1,0:T(8,128)(2,1)} fusion(bf16[512,768]{1,0:T(8,128)(2,1)S(1)} %get-tuple-element.31, bf16[512,2048]{1,0:T(8,128)(2,1)S(1)} %copy-done.13), kind=kOutput, calls=%fused_computation.11 | convolution fusion | flops 1612185600 | bytes 6029312 | tf_op jit(solution)/shard_map/dot_general | solution.py:62
  79.1 1.8 convolution_convert_fusion.4
  81.0 0.6 collective-permute-start.11
  81.6 3.4 %multiply_convert_fusion.2 = (bf16[512,768]{1,0:T(8,128)(2,1)S(1)}, f32[512,768]{1,0:T(8,128)S(1)}) fusion(f32[512]{0:T(512)S(1)} %convert_element_type.112, f32[512,768]{1,0:T(8,128)} %fusion.21, f32[512,768]{1,0:T(8,128)} %collective-permute-done.5, f32[512,768]{1,0:T(8,128)} %fusion.13, f32[512,768]{1,0:T(8,128)} %collective-permute-done.6), kind=kLoop, calls=%fused_computation.45 | loop fusion | flops 3538944 | bytes 8652800 | tf_op jit(solution)/shard_map/convert_element_type | solution.py:67
  85.0 1.8 fusion.30
  86.9 34.2 %collective-permute-done.11 = bf16[40,2048]{1,0:T(8,128)(2,1)S(1)} collective-permute-done((bf16[40,2048]{1,0:T(8,128)(2,1)S(1)}, bf16[40,2048]{1,0:T(8,128)(2,1)S(1)}, u32[]{:S(2)}, u32[]{:S(2)}) %collective-permute-start.11) | collective-permute-done | bytes 163872 | tf_op jit(solution)/shard_map/ppermute | solution.py:10
  121.0 1.9 fusion.3
  123.0 3.5 %convolution_convert_fusion.3 = bf16[768,2048]{1,0:T(8,128)(2,1)} fusion(bf16[512,768]{1,0:T(8,128)(2,1)S(1)} %get-tuple-element.33, bf16[512,2048]{1,0:T(8,128)(2,1)S(1)} %copy-done.5), kind=kOutput, calls=%fused_computation.9 | convolution fusion | flops 1612185600 | bytes 6029312 | tf_op jit(solution)/shard_map/dot_general | solution.py:62
  126.6 1.8 fusion.9
  128.4 1.8 fusion.15
  130.3 1.9 fusion.27
  132.2 3.7 %collective-permute-start.7 = (bf16[512,2048]{1,0:T(8,128)(2,1)S(1)}, bf16[512,2048]{1,0:T(8,128)(2,1)S(1)}, u32[]{:S(2)}, u32[]{:S(2)}) collective-permute-start(bf16[512,2048]{1,0:T(8,128)(2,1)S(1)} %fusion.30), channel_id=1, source_target_pairs={{0,30},{2,0},{4,2},{6,4},{8,6},{10,8},{12,10},{14,12},{16,14},{18,... | collective-permute-start | bytes 6291464 | tf_op jit(solution)/shard_map/ppermute | solution.py:10
  135.9 2.9 %multiply_convert_fusion.1 = (bf16[512,768]{1,0:T(8,128)(2,1)S(1)}, bf16[512,768]{1,0:T(8,128)(2,1)S(1)}) fusion(f32[512,768]{1,0:T(8,128)S(1)} %get-tuple-element.28, f32[512,768]{1,0:T(8,128)} %fusion.21, f32[512,768]{1,0:T(8,128)} %collective-permute-done.5, f32[512]{0:T(512)S(1)} %convert_element_type.112, f32[512,768]{1,0:T(8,128)S(1)} %fusion.3, ...), kind=kLoop, calls=%fused_computation.43 | loop fusion | flops 6291456 | bytes 9439232 | tf_op jit(solution)/shard_map/convert_element_type | solution.py:75
  138.8 1.8 fusion.11
  140.6 1.9 add_convert_fusion.4
  142.5 0.1 slice.25
  142.7 1.6 collective-permute-start.13
  144.2 0.2 copy-done.16
  144.4 3.6 %fusion.2 = bf16[1,768,2048]{2,1,0:T(8,128)(2,1)} fusion(bf16[768,2048]{1,0:T(8,128)(2,1)S(1)} %copy-done.16, bf16[512,768]{1,0:T(8,128)(2,1)S(1)} %get-tuple-element.27, bf16[40,2048]{1,0:T(8,128)(2,1)S(1)} %collective-permute-done.11, bf16[16,2048]{1,0:T(8,128)(2,1)S(1)} %broadcast_select_fusion, bf16[456,2048]{1,0:T(8,128)(2,1)S(1)} %collective-permute-done.8), kind=kOutput, calls=%fused_computation.14 | convolution fusion | flops 1624768512 | bytes 9175040 | tf_op jit(solution)/shard_map/dot_general | solution.py:62
  148.1 1.6 collective-permute-start.14
  149.6 5.2 %fusion = bf16[1,768,2048]{2,1,0:T(8,128)(2,1)} fusion(bf16[768,2048]{1,0:T(8,128)(2,1)S(1)} %copy-done.15, bf16[512,768]{1,0:T(8,128)(2,1)S(1)} %get-tuple-element.29, bf16[512,2048]{1,0:T(8,128)(2,1)} %collective-permute-done.4), kind=kOutput, calls=%fused_computation.12 | convolution fusion | flops 1618477056 | bytes 9175040 | tf_op jit(solution)/shard_map/dot_general | solution.py:62
  154.8 5.2 %fusion.1 = bf16[1,768,2048]{2,1,0:T(8,128)(2,1)} fusion(bf16[768,2048]{1,0:T(8,128)(2,1)S(1)} %convolution_convert_fusion.4, bf16[512,768]{1,0:T(8,128)(2,1)S(1)} %get-tuple-element.30, bf16[512,2048]{1,0:T(8,128)(2,1)} %collective-permute-done.4), kind=kOutput, calls=%fused_computation.13 | convolution fusion | flops 1618477056 | bytes 9175040 | tf_op jit(solution)/shard_map/dot_general | solution.py:62
  160.0 21.9 %collective-permute-done.7 = bf16[512,2048]{1,0:T(8,128)(2,1)S(1)} collective-permute-done((bf16[512,2048]{1,0:T(8,128)(2,1)S(1)}, bf16[512,2048]{1,0:T(8,128)(2,1)S(1)}, u32[]{:S(2)}, u32[]{:S(2)}) %collective-permute-start.7) | collective-permute-done | bytes 2097184 | tf_op jit(solution)/shard_map/ppermute | solution.py:10
  181.9 2.0 add_convert_fusion.5
  183.9 37.3 %collective-permute-done.13 = bf16[448,2048]{1,0:T(8,128)(2,1)S(1)} collective-permute-done((bf16[448,2048]{1,0:T(8,128)(2,1)S(1)}, bf16[448,2048]{1,0:T(8,128)(2,1)S(1)}, u32[]{:S(2)}, u32[]{:S(2)}) %collective-permute-start.13) | collective-permute-done | bytes 1835040 | tf_op jit(solution)/shard_map/ppermute | solution.py:10
  221.2 0.7 add_convert_fusion.3
  221.9 4.5 %collective-permute-done.14 = bf16[64,2048]{1,0:T(8,128)(2,1)S(1)} collective-permute-done((bf16[64,2048]{1,0:T(8,128)(2,1)S(1)}, bf16[64,2048]{1,0:T(8,128)(2,1)S(1)}, u32[]{:S(2)}, u32[]{:S(2)}) %collective-permute-start.14) | collective-permute-done | bytes 262176 | tf_op jit(solution)/shard_map/ppermute | solution.py:10
  226.4 1.3 copy-done.6
  (51 shorter events, 0.5 us)
Async XLA Ops:
  0.6 3.1 %copy-start = (bf16[1,768,2048]{2,1,0:T(8,128)(2,1)S(1)}, bf16[1,768,2048]{2,1,0:T(8,128)(2,1)}, u32[]{:S(2)}) copy-start(bf16[1,768,2048]{2,1,0:T(8,128)(2,1)} %param.17) | copy-start | bytes 9437188
  0.6 7.6 %copy-start.12 = (bf16[512,2048]{1,0:T(8,128)(2,1)S(1)}, bf16[512,2048]{1,0:T(8,128)(2,1)}, u32[]{:S(2)}) copy-start(bf16[512,2048]{1,0:T(8,128)(2,1)} %param.9) | copy-start | bytes 6291460
  0.7 7.6 %copy-start.10 = (bf16[1,768,2048]{2,1,0:T(8,128)(2,1)S(1)}, bf16[1,768,2048]{2,1,0:T(8,128)(2,1)}, u32[]{:S(2)}) copy-start(bf16[1,768,2048]{2,1,0:T(8,128)(2,1)} %param.16) | copy-start | bytes 9437188
  0.7 53.0 %collective-permute-start.4 = (bf16[512,2048]{1,0:T(8,128)(2,1)}, bf16[512,2048]{1,0:T(8,128)(2,1)}, u32[]{:S(2)}, u32[]{:S(2)}) collective-permute-start(bf16[512,2048]{1,0:T(8,128)(2,1)} %param.9), channel_id=1, source_target_pairs={{0,2},{2,4},{4,6},{6,8},{8,10},{10,12},{12,14},{14,16},{16,18},{18... | collective-permute-start | bytes 6291464 | tf_op jit(solution)/shard_map/ppermute | solution.py:10
  8.3 3.6 %copy-start.2 = (bf16[1,768,2048]{2,1,0:T(8,128)(2,1)S(1)}, bf16[1,768,2048]{2,1,0:T(8,128)(2,1)}, u32[]{:S(2)}) copy-start(bf16[1,768,2048]{2,1,0:T(8,128)(2,1)} %param.15) | copy-start | bytes 9437188
  8.3 59.4 %collective-permute-start.2 = (f32[512,768]{1,0:T(8,128)}, f32[512,768]{1,0:T(8,128)}, u32[]{:S(2)}, u32[]{:S(2)}) collective-permute-start(f32[512,768]{1,0:T(8,128)} %fusion.7), channel_id=1, source_target_pairs={{0,1},{1,0},{2,3},{3,2},{4,5},{5,4},{6,7},{7,6},{8,9},{9,8},{10,11... | collective-permute-start | bytes 4718600 | tf_op jit(solution)/shard_map/ppermute | solution.py:10
  11.3 3.6 %copy-start.14 = (s32[16]{0:T(128)S(1)}, s32[16]{0:T(128)}, u32[]{:S(2)}) copy-start(s32[16]{0:T(128)} %param.14) | copy-start | bytes 196
  11.3 4.8 %copy-start.9 = (s32[16]{0:T(128)S(1)}, s32[16]{0:T(128)}, u32[]{:S(2)}) copy-start(s32[16]{0:T(128)} %param.13) | copy-start | bytes 196
  11.3 5.5 %copy-start.7 = (s32[512,8]{0,1:T(8,128)S(1)}, s32[512,8]{0,1:T(8,128)}, u32[]{:S(2)}) copy-start(s32[512,8]{0,1:T(8,128)} %param.11) | copy-start | bytes 49156
  11.3 5.5 %copy-start.8 = (bf16[512,8]{0,1:T(8,128)(2,1)S(1)}, bf16[512,8]{0,1:T(8,128)(2,1)}, u32[]{:S(2)}) copy-start(bf16[512,8]{0,1:T(8,128)(2,1)} %param.12) | copy-start | bytes 24580
  11.3 57.7 %collective-permute-start.1 = (f32[512,768]{1,0:T(8,128)}, f32[512,768]{1,0:T(8,128)}, u32[]{:S(2)}, u32[]{:S(2)}) collective-permute-start(f32[512,768]{1,0:T(8,128)} %fusion.17), channel_id=1, source_target_pairs={{0,1},{1,0},{2,3},{3,2},{4,5},{5,4},{6,7},{7,6},{8,9},{9,8},{10,11... | collective-permute-start | bytes 4718600 | tf_op jit(solution)/shard_map/ppermute | solution.py:10
  14.8 55.5 %collective-permute-start = (f32[512,768]{1,0:T(8,128)}, f32[512,768]{1,0:T(8,128)}, u32[]{:S(2)}, u32[]{:S(2)}) collective-permute-start(f32[512,768]{1,0:T(8,128)} %fusion.25), channel_id=1, source_target_pairs={{0,1},{1,0},{2,3},{3,2},{4,5},{5,4},{6,7},{7,6},{8,9},{9,8},{10,11... | collective-permute-start | bytes 4718600 | tf_op jit(solution)/shard_map/ppermute | solution.py:10
  18.1 41.1 %copy-start.3 = (bf16[1,768,2048]{2,1,0:T(8,128)(2,1)S(1)}, bf16[1,768,2048]{2,1,0:T(8,128)(2,1)}, u32[]{:S(2)}) copy-start(bf16[1,768,2048]{2,1,0:T(8,128)(2,1)} %param.15) | copy-start | bytes 9437188
  18.1 45.7 %collective-permute-start.3 = (bf16[512]{0:T(512)(128)(2,1)S(1)}, bf16[512]{0:T(512)(128)(2,1)S(1)}, u32[]{:S(2)}, u32[]{:S(2)}) collective-permute-start(bf16[512]{0:T(512)(128)(2,1)S(1)} %multiply_convert_fusion.6), channel_id=1, source_target_pairs={{0,2},{2,4},{4,6},{6,8},{8,10},{10,12},{12,14},{14,16},{16,18},{18... | collective-permute-start | bytes 3080 | tf_op jit(solution)/shard_map/ppermute | solution.py:10
  59.2 21.8 %collective-permute-start.6 = (f32[512,768]{1,0:T(8,128)}, f32[512,768]{1,0:T(8,128)}, u32[]{:S(2)}, u32[]{:S(2)}) collective-permute-start(f32[512,768]{1,0:T(8,128)} %fusion.13), channel_id=1, source_target_pairs={{0,1},{1,0},{2,3},{3,2},{4,5},{5,4},{6,7},{7,6},{8,9},{9,8},{10,11... | collective-permute-start | bytes 4718600 | tf_op jit(solution)/shard_map/ppermute | solution.py:10
  63.8 17.9 %collective-permute-start.5 = (f32[512,768]{1,0:T(8,128)}, f32[512,768]{1,0:T(8,128)}, u32[]{:S(2)}, u32[]{:S(2)}) collective-permute-start(f32[512,768]{1,0:T(8,128)} %fusion.21), channel_id=1, source_target_pairs={{0,1},{1,0},{2,3},{3,2},{4,5},{5,4},{6,7},{7,6},{8,9},{9,8},{10,11... | collective-permute-start | bytes 4718600 | tf_op jit(solution)/shard_map/ppermute | solution.py:10
  67.7 19.1 %collective-permute-start.10 = (bf16[16,2048]{1,0:T(8,128)(2,1)S(1)}, bf16[16,2048]{1,0:T(8,128)(2,1)S(1)}, u32[]{:S(2)}, u32[]{:S(2)}) collective-permute-start(bf16[16,2048]{1,0:T(8,128)(2,1)S(1)} %slice.20), channel_id=1, source_target_pairs={{30,0},{31,1}} | collective-permute-start | bytes 196616 | tf_op jit(solution)/shard_map/ppermute | solution.py:110
  69.0 17.8 %collective-permute-start.9 = (bf16[16,2048]{1,0:T(8,128)(2,1)S(1)}, bf16[16,2048]{1,0:T(8,128)(2,1)S(1)}, u32[]{:S(2)}, u32[]{:S(2)}) collective-permute-start(bf16[16,2048]{1,0:T(8,128)(2,1)S(1)} %slice.20), channel_id=1, source_target_pairs={{0,2},{2,4},{4,6},{6,8},{8,10},{10,12},{12,14},{14,16},{16,18},{18... | collective-permute-start | bytes 196616 | tf_op jit(solution)/shard_map/ppermute | solution.py:109
  70.3 50.7 %collective-permute-start.8 = (bf16[456,2048]{1,0:T(8,128)(2,1)S(1)}, bf16[456,2048]{1,0:T(8,128)(2,1)S(1)}, u32[]{:S(2)}, u32[]{:S(2)}) collective-permute-start(bf16[456,2048]{1,0:T(8,128)(2,1)S(1)} %slice.19), channel_id=1, source_target_pairs={{0,2},{2,4},{4,6},{6,8},{8,10},{10,12},{12,14},{14,16},{16,18},{18... | collective-permute-start | bytes 5603336 | tf_op jit(solution)/shard_map/ppermute | solution.py:10
  70.7 4.9 %copy-start.13 = (bf16[512,2048]{1,0:T(8,128)(2,1)S(1)}, bf16[512,2048]{1,0:T(8,128)(2,1)}, u32[]{:S(2)}) copy-start(bf16[512,2048]{1,0:T(8,128)(2,1)} %param.9) | copy-start | bytes 6291460
  81.0 40.0 %collective-permute-start.11 = (bf16[40,2048]{1,0:T(8,128)(2,1)S(1)}, bf16[40,2048]{1,0:T(8,128)(2,1)S(1)}, u32[]{:S(2)}, u32[]{:S(2)}) collective-permute-start(bf16[40,2048]{1,0:T(8,128)(2,1)S(1)} %slice.21), channel_id=1, source_target_pairs={{0,2},{2,4},{4,6},{6,8},{8,10},{10,12},{12,14},{14,16},{16,18},{18... | collective-permute-start | bytes 491528 | tf_op jit(solution)/shard_map/ppermute | solution.py:10
  121.0 2.0 copy-start.5
  122.9 12.9 %collective-permute-start.12 = (f32[512,768]{1,0:T(8,128)S(1)}, f32[512,768]{1,0:T(8,128)S(1)}, u32[]{:S(2)}, u32[]{:S(2)}) collective-permute-start(f32[512,768]{1,0:T(8,128)S(1)} %fusion.3), channel_id=1, source_target_pairs={{0,1},{1,0},{2,3},{3,2},{4,5},{5,4},{6,7},{7,6},{8,9},{9,8},{10,11... | collective-permute-start | bytes 4718600 | tf_op jit(solution)/shard_map/ppermute | solution.py:10
  126.6 1.9 copy-start.11
  128.4 1.9 copy-start.4
  132.2 49.7 %collective-permute-start.7 = (bf16[512,2048]{1,0:T(8,128)(2,1)S(1)}, bf16[512,2048]{1,0:T(8,128)(2,1)S(1)}, u32[]{:S(2)}, u32[]{:S(2)}) collective-permute-start(bf16[512,2048]{1,0:T(8,128)(2,1)S(1)} %fusion.30), channel_id=1, source_target_pairs={{0,30},{2,0},{4,2},{6,4},{8,6},{10,8},{12,10},{14,12},{16,14},{18,... | collective-permute-start | bytes 6291464 | tf_op jit(solution)/shard_map/ppermute | solution.py:10
  142.5 1.9 copy-start.16
  142.7 7.0 %copy-start.15 = (bf16[768,2048]{1,0:T(8,128)(2,1)S(1)}, bf16[768,2048]{1,0:T(8,128)(2,1)}, u32[]{:S(2)}) copy-start(bf16[768,2048]{1,0:T(8,128)(2,1)} %convolution_convert_fusion.5) | copy-start | bytes 9437188
  142.7 78.5 %collective-permute-start.13 = (bf16[448,2048]{1,0:T(8,128)(2,1)S(1)}, bf16[448,2048]{1,0:T(8,128)(2,1)S(1)}, u32[]{:S(2)}, u32[]{:S(2)}) collective-permute-start(bf16[448,2048]{1,0:T(8,128)(2,1)S(1)} %slice.25), channel_id=1, source_target_pairs={{0,30},{2,0},{4,2},{6,4},{8,6},{10,8},{12,10},{14,12},{16,14},{18,... | collective-permute-start | bytes 5505032 | tf_op jit(solution)/shard_map/ppermute | solution.py:10
  148.1 78.3 %collective-permute-start.14 = (bf16[64,2048]{1,0:T(8,128)(2,1)S(1)}, bf16[64,2048]{1,0:T(8,128)(2,1)S(1)}, u32[]{:S(2)}, u32[]{:S(2)}) collective-permute-start(bf16[64,2048]{1,0:T(8,128)(2,1)S(1)} %slice.26), channel_id=1, source_target_pairs={{0,30},{2,0},{4,2},{6,4},{8,6},{10,8},{12,10},{14,12},{16,14},{18,... | collective-permute-start | bytes 786440 | tf_op jit(solution)/shard_map/ppermute | solution.py:10
  221.2 6.5 %copy-start.1 = (bf16[1,768,2048]{2,1,0:T(8,128)(2,1)S(1)}, bf16[1,768,2048]{2,1,0:T(8,128)(2,1)}, u32[]{:S(2)}) copy-start(bf16[1,768,2048]{2,1,0:T(8,128)(2,1)} %param.17) | copy-start | bytes 9437188
  226.4 1.3 copy-start.6
